TPU v7x, 256 devices: a whole 4x4x8 slice. The times are simulated.
256 devices in a mesh: pair: 4 (over z_lo, core), dp: 64 (over z_hi, x, y).
Axes of the slice: x: 4, y: 4, z: 8 (z_hi: 4, z_lo: 2; z = z_hi * 2 + z_lo), core: 2. Of those that a mesh axis runs over, the one named last changes fastest.
Arguments:
- master: float32 [4, 1048576], P('pair', 'dp'), may hold values from -6 to 6
- moment1: float32 [4, 1048576], P('pair', 'dp'), may hold values from -4 to 4
- moment2: float32 [4, 1048576], P('pair', 'dp'), may hold values from 0.05 to 2
- local_grad: bfloat16 [4, 64, 1048576], P('pair', 'dp'), may hold values from -16 to 16
- partner: int32 [64, 4], P('dp'), may hold values from 0 to 3, as said below
Outputs:
- new_master: float32 [4, 64, 2, 16384], P('pair', 'dp')
- new_moment1: float32 [4, 64, 2, 16384], P('pair', 'dp')
- new_moment2: float32 [4, 64, 2, 16384], P('pair', 'dp')
Inputs may be any that keep to these rules, and one draw needn't show every extreme that they name: partner[d, partner[d, i]] == i and partner[d, i] != i for every d and i: each row a perfect matching of the 4 pair indices.
All inputs are finite; a program needn't handle non-finite values.
Results may differ from a plain program's by a relative error of at most 0.0003.
Values sent between devices are 32-bit elements; how exact they have to be, the bound alone decides.
A program may use at most 64 MiB of HBM per device.

v0:
```python
import jax
import jax.numpy as jnp
from jax import lax
from jax.sharding import Mesh
from jax.sharding import PartitionSpec as P

DP = ("dp_0", "dp_1", "dp_2")


beta_one = 0.9
beta_two = 0.95
bias_one = 1.0 - 0.9**10
bias_two = 1.0 - 0.95**10
rate = 0.001
decay = 0.1
eps_value = 1e-08


def reduced_to_own(pieces, axes, order):
    shape = [lax.axis_size(a) for a in axes]
    pieces = pieces.reshape(*shape, *pieces.shape[1:])
    pieces = pieces.transpose(*order, *range(len(axes), pieces.ndim))
    pieces = pieces.reshape(-1, *pieces.shape[len(axes) :])
    for k in order:
        pieces = lax.psum_scatter(pieces, axes[k], scatter_dimension=0, tiled=True)
    return pieces[0]


def split_up(value, dim, count):
    shape = value.shape
    pieces = value.reshape(*shape[:dim], count, shape[dim] // count, *shape[dim + 1 :])
    return jnp.moveaxis(pieces, dim, 0)


def summed_rows(value, axes, order, dim):
    count = lax.axis_size(axes)
    return reduced_to_own(split_up(value, dim, count), axes, order)


def from_everyone(value, axis):
    count = lax.axis_size(axis)
    return lax.all_to_all(
        jnp.broadcast_to(value[None], (count, *value.shape)), axis, 0, 0, tiled=True
    )


def in_order(pieces, dim):
    shape = list(pieces.shape[1:])
    shape[dim] *= pieces.shape[0]
    return jnp.moveaxis(pieces, 0, dim).reshape(shape)


def gather_directly(value, axis, dim):
    pieces = from_everyone(value, axis)
    return in_order(pieces, dim)


def taken_together(value, axis):
    everything = from_everyone(value, axis)
    return jnp.sum(everything, axis=0)


def adamw_update(weights, first, second, grads, scale):
    scaled = scale * grads
    first_new = beta_one * first + (1.0 - beta_one) * scaled
    second_new = beta_two * second + (1.0 - beta_two) * scaled * scaled
    change = first_new / bias_one / (jnp.sqrt(second_new / bias_two) + eps_value) + decay * weights
    return (weights - rate * change, first_new, second_new)


def on_device(master, moment1, moment2, local_grad, partner):
    mine = lax.axis_index("pair")
    mate = partner[0, mine]
    survive = mine < mate
    n_pair = lax.axis_size("pair")
    n_dp = lax.axis_size(DP)
    shard = master.shape[1]
    count = n_pair * n_dp * shard
    term = local_grad[0, 0].astype(jnp.float32).reshape(n_dp, shard)
    reduced = summed_rows(term, DP, (1, 2, 0), 0)[0]
    packed = jnp.stack([master[0], moment1[0], moment2[0], reduced])
    whole = gather_directly(packed[None], "pair", 0)
    theirs = lax.dynamic_index_in_dim(whole, mate, 0, keepdims=False)
    grads_all = whole[:, 3]
    norm2 = taken_together(jnp.sum(grads_all * grads_all), DP)
    scale = 1.0 / jnp.maximum(jnp.sqrt(norm2 / count), 1.0)
    weights = jnp.stack([packed[0], theirs[0]])
    first = jnp.stack([packed[1], theirs[1]])
    second = jnp.stack([packed[2], theirs[2]])
    grads = jnp.stack([reduced, theirs[3]])
    results = adamw_update(weights, first, second, grads, scale)
    return tuple((jnp.where(survive, item, 0.0).reshape(1, 1, 2, shard) for item in results))


def solution(mesh):
    finer = Mesh(
        mesh.devices.reshape(mesh.shape["pair"], 4, 4, 4), ("pair", "dp_0", "dp_1", "dp_2")
    )
    in_specs = (P("pair", DP), P("pair", DP), P("pair", DP), P("pair", DP, None), P(DP, None))
    out_specs = (P("pair", DP, None, None), P("pair", DP, None, None), P("pair", DP, None, None))
    return jax.shard_map(
        on_device, mesh=finer, in_specs=in_specs, out_specs=out_specs, check_vma=False
    )
```

profile of v0, /device:TPU:1, one launch (start us, length us, event | category | flops | bytes accessed | tf_op | source)
XLA Modules:
  0.0 323.2 jit_solution(18110794317501675407)
XLA Ops:
  7.2 0.0 copy-start
  7.2 0.0 all-reduce.7.cloned.1.call-start
  7.2 37.8 %convert_reduce_fusion = f32[1048576]{0:T(1024)} fusion(bf16[1,1,1048576]{2,1,0:T(2,128)(2,1)} %param.8), kind=kLoop, calls=%fused_computation | loop fusion | flops 1048576 | bytes 6291456 | tf_op jit(solution)/shard_map/reshape | solution.py:23
  45.0 5.6 %reshape.284 = f32[4,4,4,1,16384]{4,2,1,0,3:T(4,128)} reshape(f32[1048576]{0:T(1024)} %convert_reduce_fusion) | data formatting | bytes 8388608 | tf_op jit(solution)/shard_map/reshape | solution.py:23
  50.6 8.5 %copy.11 = f32[4,4,4,1,16384]{4,3,0,2,1:T(1,128)} copy(f32[4,4,4,1,16384]{4,2,1,0,3:T(4,128)} %reshape.284) | data formatting | bytes 8388608 | tf_op jit(solution)/shard_map/reshape | solution.py:23
  59.1 0.0 copy-start.6
  59.1 0.0 copy-start.5
  59.1 0.0 copy-start.4
  59.1 0.0 copy-start.1
  59.1 0.0 copy-start.2
  59.2 0.0 copy-start.3
  59.2 0.0 all-reduce.7.cloned.1.call-update
  59.2 0.0 all-reduce.9.cloned.1.call-start
  59.2 0.6 copy-done.6
  59.8 0.6 dynamic-slice.1
  61.0 99.8 %all-reduce.7.cloned.1.call-done = f32[64,1,16384]{2,1,0:T(1,128)} async-done(((f32[64,1,16384]{2,1,0:T(1,128)}), f32[64,1,16384]{2,1,0:T(1,128)}) %all-reduce.7.cloned.1.call-update) | async-done | bytes 4194320
  160.8 2.3 constant_dynamic-slice_fusion.6
  163.1 0.0 all-reduce.9.cloned.1.call-update
  163.1 0.0 all-reduce.11.cloned.1.call-start
  163.2 0.0 copy-done.5
  163.2 0.6 dynamic-slice.3
  164.4 48.3 %all-reduce.9.cloned.1.call-done = f32[16,1,16384]{2,1,0:T(1,128)} async-done(((f32[16,1,16384]{2,1,0:T(1,128)}), f32[16,1,16384]{2,1,0:T(1,128)}) %all-reduce.9.cloned.1.call-update) | async-done | bytes 1048592
  212.8 1.7 constant_dynamic-slice_fusion.5
  214.4 0.0 all-reduce.11.cloned.1.call-update
  214.5 0.0 copy-done.4
  214.5 0.6 dynamic-slice.5
  215.1 52.1 %all-reduce.11.cloned.1.call-done = f32[4,1,16384]{2,1,0:T(1,128)} async-done(((f32[4,1,16384]{2,1,0:T(1,128)}), f32[4,1,16384]{2,1,0:T(1,128)}) %all-reduce.11.cloned.1.call-update) | async-done | bytes 262160
  267.2 1.6 dynamic-slice_bitcast_fusion
  268.8 0.0 copy-done.1
  268.8 0.0 copy-done.2
  268.8 0.0 copy-done.3
  268.8 0.3 pad_maximum_fusion
  269.1 1.1 broadcast_in_dim.17
  270.2 6.3 %all-to-all-start = ((f32[4,1,4,16384]{3,2,1,0:T(4,128)}), f32[4,1,4,16384]{3,2,1,0:T(4,128)S(1)}, u32[]{:S(2)}, u32[]{:S(2)}) async-start(f32[4,1,4,16384]{3,2,1,0:T(4,128)} %broadcast_in_dim.17), calls=%async_computation | async-start | bytes 2097152 | tf_op jit(solution)/shard_map/all_to_all | solution.py:42
  276.5 0.0 copy-done
  276.5 0.6 constant_dynamic-slice_fusion.4
  279.7 10.3 %all-to-all-done = f32[4,1,4,16384]{3,2,1,0:T(4,128)S(1)} async-done(((f32[4,1,4,16384]{3,2,1,0:T(4,128)}), f32[4,1,4,16384]{3,2,1,0:T(4,128)S(1)}, u32[]{:S(2)}, u32[]{:S(2)}) %all-to-all-start) | async-done | bytes 1048608 | tf_op jit(solution)/shard_map/all_to_all | solution.py:42
  290.0 1.1 fusion
  291.1 1.3 broadcast_in_dim.18
  292.4 10.0 %all-to-all-start.1 = ((f32[64,1,1]{2,1,0:T(1,128)}), f32[64,1,1]{2,1,0:T(1,128)S(1)}, u32[]{:S(2)}, u32[]{:S(2)}) async-start(f32[64,1,1]{2,1,0:T(1,128)} %broadcast_in_dim.18), calls=%async_computation.1 | async-start | bytes 65536 | tf_op jit(solution)/shard_map/all_to_all | solution.py:42
  302.4 0.2 constant_dynamic-slice_fusion.1
  302.6 10.4 %all-to-all-done.1 = f32[64,1,1]{2,1,0:T(1,128)S(1)} async-done(((f32[64,1,1]{2,1,0:T(1,128)}), f32[64,1,1]{2,1,0:T(1,128)S(1)}, u32[]{:S(2)}, u32[]{:S(2)}) %all-to-all-start.1) | async-done | bytes 288 | tf_op jit(solution)/shard_map/all_to_all | solution.py:42
  313.0 0.7 reduce_sum.19
  314.4 1.2 broadcast_select_fusion.1
  315.6 1.0 subtract_select_fusion
Async XLA Ops:
  7.2 269.3 %copy-start = (s32[1,4]{1,0:T(1,128)S(1)}, s32[1,4]{1,0:T(1,128)}, u32[]{:S(2)}) copy-start(s32[1,4]{1,0:T(1,128)} %param.9) | copy-start | bytes 52
  7.2 153.6 %all-reduce.7.cloned.1.call-start = ((), (), s32[]{:S(2)}) async-start(), calls=%async_computation.2 | async-start | bytes 8388608
  59.1 0.7 copy-start.6
  59.1 104.1 %copy-start.5 = (u32[256]{0:T(256)S(1)}, u32[256]{0:T(256)}, u32[]{:S(2)}) copy-start(u32[256]{0:T(256)} %constant.51) | copy-start | bytes 3076
  59.1 155.3 %copy-start.4 = (u32[256]{0:T(256)S(1)}, u32[256]{0:T(256)}, u32[]{:S(2)}) copy-start(u32[256]{0:T(256)} %constant.55) | copy-start | bytes 3076
  59.1 209.6 %copy-start.1 = (f32[1,16384]{1,0:T(1,128)S(1)}, f32[1,16384]{1,0:T(1,128)}, u32[]{:S(2)}) copy-start(f32[1,16384]{1,0:T(1,128)} %param.7) | copy-start | bytes 196612
  59.1 209.6 %copy-start.2 = (f32[1,16384]{1,0:T(1,128)S(1)}, f32[1,16384]{1,0:T(1,128)}, u32[]{:S(2)}) copy-start(f32[1,16384]{1,0:T(1,128)} %param.6) | copy-start | bytes 196612
  59.2 209.6 %copy-start.3 = (f32[1,16384]{1,0:T(1,128)S(1)}, f32[1,16384]{1,0:T(1,128)}, u32[]{:S(2)}) copy-start(f32[1,16384]{1,0:T(1,128)} %param.5) | copy-start | bytes 196612
  59.2 153.6 %all-reduce.9.cloned.1.call-start = ((), (), s32[]{:S(2)}) async-start(), calls=%async_computation.3 | async-start | bytes 2097152
  163.1 104.1 %all-reduce.11.cloned.1.call-start = ((), (), s32[]{:S(2)}) async-start(), calls=%async_computation.4 | async-start | bytes 524288
  270.2 19.8 %all-to-all-start = ((f32[4,1,4,16384]{3,2,1,0:T(4,128)}), f32[4,1,4,16384]{3,2,1,0:T(4,128)S(1)}, u32[]{:S(2)}, u32[]{:S(2)}) async-start(f32[4,1,4,16384]{3,2,1,0:T(4,128)} %broadcast_in_dim.17), calls=%async_computation | async-start | bytes 2097152 | tf_op jit(solution)/shard_map/all_to_all | solution.py:42
  292.4 20.6 %all-to-all-start.1 = ((f32[64,1,1]{2,1,0:T(1,128)}), f32[64,1,1]{2,1,0:T(1,128)S(1)}, u32[]{:S(2)}, u32[]{:S(2)}) async-start(f32[64,1,1]{2,1,0:T(1,128)} %broadcast_in_dim.18), calls=%async_computation.1 | async-start | bytes 65536 | tf_op jit(solution)/shard_map/all_to_all | solution.py:42
Sparse Core Ops, SparseCore 0:
  59.3 101.4 all-reduce.6
  163.3 49.4 all-reduce.8
  215.4 51.7 all-reduce.10
where the time goes:
time: 324 us; the launch traced here: 323 us
  waiting for transfers between devices  221 us (68%)
  other arithmetic  42.1 us (13%)
  local copies, waits for them, and re-layouts  25.2 us (8%)
  between operations  18.5 us (6%)
  starting transfers between devices  16.4 us (5%)
    unnamed x6, waiting for transfers between devices  200 us
    reshape x1, other arithmetic, reduced_to_own(): pieces = pieces.reshape(-1, *pieces.shape[len(axes):])  37.8 us
    all_to_all x2, waiting for transfers between devices, from_everyone(): lax.all_to_all(jnp.broadcast_to(value[None], (count, *value.shape)), axis...  20.7 us
    all_to_all x2, starting transfers between devices, from_everyone(): lax.all_to_all(jnp.broadcast_to(value[None], (count, *value.shape)), axis...  16.3 us
    reshape x2, local copies, waits for them, and re-layouts, reduced_to_own(): pieces = pieces.reshape(-1, *pieces.shape[len(axes):])  14.1 us
  transfers between devices with their start and end apart: 5, of which 5 were waited for; matrix products, arithmetic and copies ran while one was open for 1% of the time, Pallas kernels for 0%

commit v1 on v0

v1 whole, which is shorter than its diff:
```python
import functools

import jax
import jax.numpy as jnp
from jax import lax
from jax.experimental import pallas as pl
from jax.experimental.pallas import tpu as pltpu
from jax.sharding import Mesh
from jax.sharding import PartitionSpec as P

beta_one = 0.9
beta_two = 0.95
bias_one = 1.0 - 0.9**10
bias_two = 1.0 - 0.95**10
rate = 0.001
decay = 0.1
eps_value = 1e-08

SH = 16384
N_DP = 64
PAIR = ("zl", "core")
DP = ("zh", "x", "y")
STRIDE = {"zh": 16, "x": 4, "y": 1}
MESH = pl.DeviceIdType.MESH

PARTS = (
    (("x", "y", "zh"), 0, 56, 32),
    (("y", "x", "zh"), 56, 56, 32),
    (("zh", "x", "y"), 112, 16, 8),
)
FIRST = (2, 0, 1)
AP, AM, BP, BM, CP, CM = range(6)


def kernel(
    partner, w_hbm, m_hbm, v_hbm, g_hbm, out_w, out_m, out_v,
    stage, own, cand, grads, cand_g, near, far,
    f0, f1, f2, r0, r1, r2, s0, s1, s2, q0, q1, q2, t0, t1, t2, u0, u1, u2,
    load_sem, own_sem, ring_send, ring_recv, pair_send, pair_recv, near_send, near_recv, far_send, far_recv,
):
    data = ((f0, s0, t0), (f1, s1, t1), (f2, s2, t2))
    landing = ((r0, q0, u0), (r1, q1, u1), (r2, q2, u2))
    at = {a: lax.axis_index(a) for a in PAIR + DP}

    def beside(axis, step):
        return lax.rem(at[axis] + step + 4, 4)

    loads = [
        pltpu.make_async_copy(
            g_hbm.at[0, :, pl.ds(i * (N_DP // 4) * SH, (N_DP // 4) * SH)],
            stage.at[:, pl.ds(i * (N_DP // 4) * SH, (N_DP // 4) * SH)],
            load_sem.at[i],
        )
        for i in range(4)
    ]
    owns = [pltpu.make_async_copy(ref, own.at[i], own_sem.at[i]) for i, ref in enumerate((w_hbm, m_hbm, v_hbm))]
    for c in loads + owns:
        c.start()
    barrier = pltpu.get_barrier_semaphore()
    near_ids = [
        {"zh": beside("zh", k // 4), "zl": lax.rem(at["zl"] + (k // 2) % 2, 2), "core": lax.rem(at["core"] + k % 2, 2)}
        for k in range(16)
    ]
    far_ids = [{"x": beside("x", k // 4), "y": beside("y", k % 4)} for k in range(16)]
    for k in range(1, 16):
        pl.semaphore_signal(barrier, inc=1, device_id=near_ids[k], device_id_type=MESH)
        pl.semaphore_signal(barrier, inc=1, device_id=far_ids[k], device_id_type=MESH)

    def convert(part, c0, half):
        order, row, rows, _ = PARTS[part]
        dst = data[part][0]

        def body(i, carry):
            c1 = half * 2 + i // 4
            c2 = lax.rem(i, 4)
            block = c0 * STRIDE[order[0]] + c1 * STRIDE[order[1]] + c2 * STRIDE[order[2]]
            for j in range(rows // 8):
                piece = stage[0:1, pl.ds(pl.multiple_of(block * SH + (row + 8 * j) * 128, 1024), 1024)]
                dst[c0, c1, c2, pl.ds(8 * j, 8), :] = piece.astype(jnp.float32).reshape(8, 128)
            return carry

        lax.fori_loop(0, 8, body, 0)

    def view(part, phase, c, half):
        ref = data[part][phase]
        if phase < 2:
            return ref.at[c, pl.ds(2 * half, 2)]
        cut, rows = PARTS[part][3], PARTS[part][2]
        return ref.at[c, pl.ds(0, cut)] if half == 0 else ref.at[c, pl.ds(cut, rows - cut)]

    def landed(part, phase, kind, half):
        ref = landing[part][phase].at[kind]
        if phase < 2:
            return ref
        cut, rows = PARTS[part][3], PARTS[part][2]
        return ref.at[pl.ds(0, cut if half == 0 else rows - cut)]

    HALF = {AP: 0, AM: 1, BP: 1, BM: 0, CP: 0, CM: 1}
    CHUNK = {AP: 2, AM: -2, BP: 1, BM: -1, CP: 1, CM: -1}

    def ring(part, phase, kind):
        axis = PARTS[part][0][phase]
        n = (part * 3 + phase) * 6 + kind
        return pltpu.make_async_remote_copy(
            src_ref=view(part, phase, beside(axis, CHUNK[kind]), HALF[kind]),
            dst_ref=landed(part, phase, kind, HALF[kind]),
            send_sem=ring_send.at[n],
            recv_sem=ring_recv.at[n],
            device_id={axis: beside(axis, 1 if kind in (AP, BP, CP) else -1)},
            device_id_type=MESH,
        )

    def flat(ref):
        shape = ref.shape
        rows = shape[-2] // 8
        lead = [()]
        for n in shape[:-2]:
            lead = [i + (j,) for i in lead for j in range(n)]
        return lead, rows

    def add_up(dst, *srcs):
        lead, rows = flat(dst)
        if len(lead) > 2:
            n1 = dst.shape[1]

            def body(i, carry):
                idx = (i // n1, lax.rem(i, n1))
                for j in range(rows):
                    tile = idx + (pl.ds(8 * j, 8), slice(None))
                    total = srcs[0][tile]
                    for s in srcs[1:]:
                        total = total + s[tile]
                    dst[tile] = total
                return carry

            lax.fori_loop(0, len(lead), body, 0)
        else:
            for idx in lead:
                for j in range(rows):
                    tile = idx + (pl.ds(8 * j, 8), slice(None))
                    total = srcs[0][tile]
                    for s in srcs[1:]:
                        total = total + s[tile]
                    dst[tile] = total

    def open_phase(part, phase):
        for kind in (AP, AM, BP, BM):
            ring(part, phase, kind).start()

    def forward(part, phase):
        axis = PARTS[part][0][phase]
        for a, c in ((AP, CP), (AM, CM)):
            ring(part, phase, a).wait_recv()
            mine = view(part, phase, beside(axis, CHUNK[c]), HALF[c])
            add_up(mine, mine, landed(part, phase, a, HALF[a]))
            ring(part, phase, c).start()

    def close_phase(part, phase):
        axis = PARTS[part][0][phase]
        for kind in (BP, BM, CP, CM):
            ring(part, phase, kind).wait_recv()
        for half, b, c in ((0, BM, CP), (1, BP, CM)):
            srcs = (
                view(part, phase, at[axis], half),
                landed(part, phase, b, half),
                landed(part, phase, c, half),
            )
            if phase < 2:
                add_up(data[part][phase + 1].at[pl.ds(2 * half, 2)], *srcs)
            else:
                row, rows, cut = PARTS[part][1:]
                lo, n = (0, cut) if half == 0 else (cut, rows - cut)
                add_up(grads.at[pl.ds(row + lo, n)], *srcs)

    for c in loads:
        c.wait()
    for part in FIRST:
        axis = PARTS[part][0][0]
        convert(part, beside(axis, 2), 0)
        convert(part, beside(axis, 2), 1)
    pl.semaphore_wait(barrier, 30)
    for part in FIRST:
        ring(part, 0, AP).start()
        ring(part, 0, AM).start()
    for part in FIRST:
        axis = PARTS[part][0][0]
        convert(part, beside(axis, 1), 1)
        convert(part, beside(axis, -1), 0)
        ring(part, 0, BP).start()
        ring(part, 0, BM).start()
    for part in FIRST:
        axis = PARTS[part][0][0]
        convert(part, beside(axis, 1), 0)
        convert(part, beside(axis, -1), 1)
        convert(part, at[axis], 0)
        convert(part, at[axis], 1)
    for part in FIRST:
        forward(part, 0)

    def pair_copy(src, dst, n, axis):
        return pltpu.make_async_remote_copy(
            src_ref=src, dst_ref=dst, send_sem=pair_send.at[n], recv_sem=pair_recv.at[n],
            device_id={axis: 1 - at[axis]}, device_id_type=MESH,
        )

    for c in owns:
        c.wait()
    shard_1 = pair_copy(own, cand.at[0], 0, "core")
    shard_2 = pair_copy(own, cand.at[1], 1, "zl")
    shard_3 = pair_copy(cand.at[1], cand.at[2], 2, "core")
    shard_1.start()
    shard_2.start()

    for phase in (0, 1, 2):
        for part in FIRST:
            close_phase(part, phase)
            if phase < 2:
                open_phase(part, phase + 1)
        if phase < 2:
            for part in FIRST:
                forward(part, phase + 1)
        if phase == 0:
            shard_2.wait_recv()
            shard_3.start()

    def squares(i, total):
        tile = grads[pl.ds(pl.multiple_of(i * 8, 8), 8), :]
        return total + tile * tile

    total = lax.fori_loop(0, 16, squares, jnp.zeros((8, 128), jnp.float32))
    near[0] = jnp.sum(total, axis=0, keepdims=True)

    def spread(buf, k, ids, send, recv):
        return pltpu.make_async_remote_copy(
            src_ref=buf.at[0], dst_ref=buf.at[k], send_sem=send.at[k], recv_sem=recv.at[k],
            device_id=ids[k], device_id_type=MESH,
        )

    near_copies = [spread(near, k, near_ids, near_send, near_recv) for k in range(1, 16)]
    far_copies = [spread(far, k, far_ids, far_send, far_recv) for k in range(1, 16)]
    grads_1 = pair_copy(grads, cand_g.at[0], 3, "core")
    grads_2 = pair_copy(grads, cand_g.at[1], 4, "zl")
    grads_3 = pair_copy(cand_g.at[1], cand_g.at[2], 5, "core")
    for c in near_copies:
        c.start()
    grads_1.start()
    grads_2.start()
    for c in near_copies:
        c.wait_recv()
    far[0] = functools.reduce(jnp.add, [near[k] for k in range(16)])
    for c in far_copies:
        c.start()
    grads_2.wait_recv()
    grads_3.start()
    for c in far_copies:
        c.wait_recv()
    norm2 = jnp.sum(functools.reduce(jnp.add, [far[k] for k in range(16)]), axis=1, keepdims=True)
    scale = 1.0 / jnp.maximum(jnp.sqrt(norm2 / (4 * N_DP * SH)), 1.0)

    shard_1.wait_recv()
    shard_3.wait_recv()
    grads_1.wait_recv()
    grads_3.wait_recv()
    mine = at["zl"] * 2 + at["core"]
    mate = partner[0, mine]
    apart = jnp.full((1, 1024), mine ^ mate, jnp.int32)
    is_one, is_two = apart == 1, apart == 2
    survive = jnp.full((1, 1024), mate - mine, jnp.int32) > 0

    def update(i, carry):
        cols = pl.ds(pl.multiple_of(i * 1024, 1024), 1024)
        rows = pl.ds(pl.multiple_of(i * 8, 8), 8)

        def chosen(one, two, three):
            return jnp.where(is_one, one, jnp.where(is_two, two, three))

        for slot in (0, 1):
            if slot == 0:
                weights, first, second = [own[a, :, cols] for a in range(3)]
                total = grads[rows, :].reshape(1, 1024)
            else:
                weights, first, second = [chosen(*[cand[k, a, :, cols] for k in range(3)]) for a in range(3)]
                total = chosen(*[cand_g[k, rows, :].reshape(1, 1024) for k in range(3)])
            scaled = scale * total
            first_new = beta_one * first + (1.0 - beta_one) * scaled
            second_new = beta_two * second + (1.0 - beta_two) * scaled * scaled
            change = first_new / bias_one / (jnp.sqrt(second_new / bias_two) + eps_value) + decay * weights
            for ref, value in ((out_w, weights - rate * change), (out_m, first_new), (out_v, second_new)):
                ref[0, 0, slot : slot + 1, cols] = jnp.where(survive, value, 0.0)
        return carry

    lax.fori_loop(0, 16, update, 0)

    for part in range(3):
        for phase in range(3):
            for kind in range(6):
                ring(part, phase, kind).wait_send()
    for c in [shard_1, shard_2, shard_3, grads_1, grads_2, grads_3] + near_copies + far_copies:
        c.wait_send()


def on_device(master, moment1, moment2, local_grad, partner):
    f32 = jnp.float32
    vmem = [pltpu.VMEM((4, 4, 4, p[2], 128), f32) for p in PARTS]
    vmem += [pltpu.VMEM((6, 2, 4, p[2], 128), f32) for p in PARTS]
    vmem += [pltpu.VMEM((4, 4, p[2], 128), f32) for p in PARTS]
    vmem += [pltpu.VMEM((6, 2, p[2], 128), f32) for p in PARTS]
    vmem += [pltpu.VMEM((4, p[2], 128), f32) for p in PARTS]
    vmem += [pltpu.VMEM((6, p[3], 128), f32) for p in PARTS]
    dma = pltpu.SemaphoreType.DMA
    out = jax.ShapeDtypeStruct((1, 1, 2, SH), f32)
    return pl.pallas_call(
        kernel,
        out_shape=(out, out, out),
        in_specs=[pl.BlockSpec(memory_space=pltpu.SMEM)] + [pl.BlockSpec(memory_space=pltpu.HBM)] * 4,
        out_specs=[pl.BlockSpec(memory_space=pltpu.VMEM)] * 3,
        scratch_shapes=[
            pltpu.VMEM((1, N_DP * SH), jnp.bfloat16),
            pltpu.VMEM((3, 1, SH), f32),
            pltpu.VMEM((3, 3, 1, SH), f32),
            pltpu.VMEM((128, 128), f32),
            pltpu.VMEM((3, 128, 128), f32),
            pltpu.VMEM((16, 1, 128), f32),
            pltpu.VMEM((16, 1, 128), f32),
        ]
        + vmem
        + [dma((4,)), dma((3,)), dma((54,)), dma((54,)), dma((6,)), dma((6,))]
        + [dma((16,))] * 4,
        compiler_params=pltpu.CompilerParams(collective_id=0, has_side_effects=True),
        name="step",
    )(partner, master, moment1, moment2, local_grad)


def solution(mesh):
    finer = Mesh(mesh.devices.reshape(2, 2, 4, 4, 4), PAIR + DP)
    in_specs = (P(PAIR, DP), P(PAIR, DP), P(PAIR, DP), P(PAIR, DP, None), P(DP, None))
    out_specs = (P(PAIR, DP, None, None),) * 3
    return jax.shard_map(on_device, mesh=finer, in_specs=in_specs, out_specs=out_specs, check_vma=False)
```

time: 324 us -> 62.2 us (0.19)
  waiting for transfers between devices: 221 us -> 0 us
  Pallas kernels: 0 us -> 56.7 us
  other arithmetic: 42.1 us -> 0 us
  local copies, waits for them, and re-layouts: 25.2 us -> 4.7 us
  between operations: 18.5 us -> 0.64 us
  starting transfers between devices: 16.4 us -> 0 us
    unnamed x6 -> x0, waiting for transfers between devices: 200 us -> none
    pallas_call x0 -> x1, Pallas kernels: none -> 56.7 us  [on_device(): pl.pallas_call(kernel, out_shape=(out, out, out), in_specs=[pl.BlockSpec(...]
    reshape x1 -> x0, other arithmetic: 37.8 us -> none  [reduced_to_own(): pieces = pieces.reshape(-1, *pieces.shape[len(axes):])]
    all_to_all x2 -> x0, waiting for transfers between devices: 20.7 us -> none  [from_everyone(): lax.all_to_all(jnp.broadcast_to(value[None], (count, *value.shape)), axis...]
    all_to_all x2 -> x0, starting transfers between devices: 16.3 us -> none  [from_everyone(): lax.all_to_all(jnp.broadcast_to(value[None], (count, *value.shape)), axis...]
    reshape x2 -> x0, local copies, waits for them, and re-layouts: 14.1 us -> none  [reduced_to_own(): pieces = pieces.reshape(-1, *pieces.shape[len(axes):])]
  transfers between devices with their start and end apart: 5 -> 0, of which waited for: 5 -> 0; matrix products, arithmetic and copies ran while one was open for 1% -> 0% of each run, Pallas kernels for 0% -> 0%
where the time goes in v1:
time: 62.2 us; the launch traced here: 62.1 us
  Pallas kernels  56.7 us (91%)
  local copies, waits for them, and re-layouts  4.7 us (8%)
  between operations  0.64 us (1%)
    pallas_call x1, Pallas kernels, on_device(): pl.pallas_call(kernel, out_shape=(out, out, out), in_specs=[pl.BlockSpec(...  56.7 us
    unnamed x3, local copies, waits for them, and re-layouts  4.7 us

profile of v1, /device:TPU:1, one launch (start us, length us, event | category | flops | bytes accessed | tf_op | source)
XLA Modules:
  0.0 62.1 jit_solution(1804091110931595381)
XLA Ops:
  0.6 56.7 %step.1 = (f32[1,1,2,16384]{3,2,1,0:T(2,128)}, f32[1,1,2,16384]{3,2,1,0:T(2,128)}, f32[1,1,2,16384]{3,2,1,0:T(2,128)}) custom-call(s32[1,4]{1,0:T(1,128)} %partner.1, f32[1,16384]{1,0:T(1,128)} %w_hbm.1, f32[1,16384]{1,0:T(1,128)} %m_hbm.1, f32[1,16384]{1,0:T(1,128)} %v_hbm.1, bf16[1,1,1048576]{2,1,0:T(2,128)(2,1)} %g_hbm.1), custom_call_target="tpu_custom_call" | custom-call | tf_op jit(solution)/shard_map/step/pallas_call | solution.py:312
  57.4 1.6 %copy.11 = f32[1,1,2,16384]{3,2,1,0:T(2,128)} copy(f32[1,1,2,16384]{3,2,1,0:T(2,128)} %get-tuple-element.6) | data formatting | bytes 262144
  58.9 1.6 %copy.12 = f32[1,1,2,16384]{3,2,1,0:T(2,128)} copy(f32[1,1,2,16384]{3,2,1,0:T(2,128)} %get-tuple-element.7) | data formatting | bytes 262144
  60.5 1.6 %copy.13 = f32[1,1,2,16384]{3,2,1,0:T(2,128)} copy(f32[1,1,2,16384]{3,2,1,0:T(2,128)} %get-tuple-element.8) | data formatting | bytes 262144

commit v2 on v1

--- a/solution.py
+++ b/solution.py
@@ -33,10 +33,10 @@
 
 
 def kernel(
-    partner, w_hbm, m_hbm, v_hbm, g_hbm, out_w, out_m, out_v,
+    partner, w_hbm, m_hbm, v_hbm, g_hbm, state, squares_sum,
     stage, own, cand, grads, cand_g, near, far,
     f0, f1, f2, r0, r1, r2, s0, s1, s2, q0, q1, q2, t0, t1, t2, u0, u1, u2,
-    load_sem, own_sem, ring_send, ring_recv, pair_send, pair_recv, near_send, near_recv, far_send, far_recv,
+    load_sem, own_sem, ring_send, ring_recv, pair_send, pair_recv, norm_send, norm_recv,
 ):
     data = ((f0, s0, t0), (f1, s1, t1), (f2, s2, t2))
     landing = ((r0, q0, u0), (r1, q1, u1), (r2, q2, u2))
@@ -45,17 +45,18 @@
     def beside(axis, step):
         return lax.rem(at[axis] + step + 4, 4)
 
-    loads = [
-        pltpu.make_async_copy(
-            g_hbm.at[0, :, pl.ds(i * (N_DP // 4) * SH, (N_DP // 4) * SH)],
-            stage.at[:, pl.ds(i * (N_DP // 4) * SH, (N_DP // 4) * SH)],
-            load_sem.at[i],
-        )
-        for i in range(4)
-    ]
-    owns = [pltpu.make_async_copy(ref, own.at[i], own_sem.at[i]) for i, ref in enumerate((w_hbm, m_hbm, v_hbm))]
-    for c in loads + owns:
-        c.start()
+    groups = (2, 1, -1, 0)
+    for i in groups:
+        for zh in range(4):
+            cols = pl.ds((zh * 16 + beside("x", i) * 4) * SH, 4 * SH)
+            pltpu.make_async_copy(g_hbm.at[0, :, cols], stage.at[:, cols], load_sem.at[i % 4]).start()
+    for i, ref in enumerate((w_hbm, m_hbm, v_hbm)):
+        pltpu.make_async_copy(ref, own.at[i], own_sem).start()
+
+    def loaded(i):
+        part_of = stage.at[:, pl.ds(0, 16 * SH)]
+        pltpu.make_async_copy(part_of, part_of, load_sem.at[i % 4]).wait()
+
     barrier = pltpu.get_barrier_semaphore()
     near_ids = [
         {"zh": beside("zh", k // 4), "zl": lax.rem(at["zl"] + (k // 2) % 2, 2), "core": lax.rem(at["core"] + k % 2, 2)}
@@ -100,15 +101,18 @@
 
     def ring(part, phase, kind):
         axis = PARTS[part][0][phase]
-        n = (part * 3 + phase) * 6 + kind
+        n = part * 3 + phase
         return pltpu.make_async_remote_copy(
             src_ref=view(part, phase, beside(axis, CHUNK[kind]), HALF[kind]),
             dst_ref=landed(part, phase, kind, HALF[kind]),
             send_sem=ring_send.at[n],
-            recv_sem=ring_recv.at[n],
+            recv_sem=ring_recv.at[n * 3 + min(kind, BP)],
             device_id={axis: beside(axis, 1 if kind in (AP, BP, CP) else -1)},
             device_id_type=MESH,
         )
+
+    def wait_bytes(ref, sem):
+        pltpu.make_async_copy(ref, ref, sem).wait()
 
     def flat(ref):
         shape = ref.shape
@@ -157,8 +161,8 @@
 
     def close_phase(part, phase):
         axis = PARTS[part][0][phase]
-        for kind in (BP, BM, CP, CM):
-            ring(part, phase, kind).wait_recv()
+        last = data[part][2].at[pl.ds(0, 2)]
+        wait_bytes(last if phase == 2 else landing[part][phase].at[pl.ds(2, 4)], ring_recv.at[(part * 3 + phase) * 3 + BP])
         for half, b, c in ((0, BM, CP), (1, BP, CM)):
             srcs = (
                 view(part, phase, at[axis], half),
@@ -172,17 +176,17 @@
                 lo, n = (0, cut) if half == 0 else (cut, rows - cut)
                 add_up(grads.at[pl.ds(row + lo, n)], *srcs)
 
-    for c in loads:
-        c.wait()
-    for part in FIRST:
+    for part in (0, 1, 2):
         axis = PARTS[part][0][0]
+        for i in groups[:1] if part == 0 else groups[1:] if part == 1 else ():
+            loaded(i)
         convert(part, beside(axis, 2), 0)
         convert(part, beside(axis, 2), 1)
-    pl.semaphore_wait(barrier, 30)
-    for part in FIRST:
+        if part == 0:
+            pl.semaphore_wait(barrier, 30)
         ring(part, 0, AP).start()
         ring(part, 0, AM).start()
-    for part in FIRST:
+    for part in (0, 1, 2):
         axis = PARTS[part][0][0]
         convert(part, beside(axis, 1), 1)
         convert(part, beside(axis, -1), 0)
@@ -199,17 +203,39 @@
 
     def pair_copy(src, dst, n, axis):
         return pltpu.make_async_remote_copy(
-            src_ref=src, dst_ref=dst, send_sem=pair_send.at[n], recv_sem=pair_recv.at[n],
+            src_ref=src, dst_ref=dst, send_sem=pair_send.at[n // 2], recv_sem=pair_recv.at[n],
             device_id={axis: 1 - at[axis]}, device_id_type=MESH,
         )
 
-    for c in owns:
-        c.wait()
+    wait_bytes(own, own_sem)
     shard_1 = pair_copy(own, cand.at[0], 0, "core")
-    shard_2 = pair_copy(own, cand.at[1], 1, "zl")
-    shard_3 = pair_copy(cand.at[1], cand.at[2], 2, "core")
+    shard_2 = pair_copy(own, cand.at[2], 1, "zl")
+    shard_3 = pair_copy(cand.at[2], cand.at[1], 0, "core")
     shard_1.start()
     shard_2.start()
+
+    mine = at["zl"] * 2 + at["core"]
+    mate = partner[0, mine]
+    apart = jnp.full((1, 1024), mine ^ mate, jnp.int32)
+    is_one, is_two = apart == 1, apart == 2
+    survive = jnp.full((1, 1024), mate - mine, jnp.int32) > 0
+
+    def keep(a, cols, value, values):
+        theirs = jnp.where(is_one, values[0], jnp.where(is_two, values[1], values[2]))
+        state[a, 0:1, cols] = jnp.where(survive, value, 0.0)
+        state[a, 1:2, cols] = jnp.where(survive, theirs, 0.0)
+
+    def choose(i, carry):
+        cols = pl.ds(pl.multiple_of(i * 1024, 1024), 1024)
+        for a in range(3):
+            keep(a, cols, own[a, :, cols], [cand[k, a, :, cols] for k in (0, 2, 1)])
+        return carry
+
+    def choose_grads(i, carry):
+        cols = pl.ds(pl.multiple_of(i * 1024, 1024), 1024)
+        rows = pl.ds(pl.multiple_of(i * 8, 8), 8)
+        keep(3, cols, grads[rows, :].reshape(1, 1024), [cand_g[k, rows, :].reshape(1, 1024) for k in (0, 2, 1)])
+        return carry
 
     for phase in (0, 1, 2):
         for part in FIRST:
@@ -222,6 +248,9 @@
         if phase == 0:
             shard_2.wait_recv()
             shard_3.start()
+        if phase == 1:
+            wait_bytes(cand.at[pl.ds(0, 2)], pair_recv.at[0])
+            lax.fori_loop(0, 16, choose, 0)
 
     def squares(i, total):
         tile = grads[pl.ds(pl.multiple_of(i * 8, 8), 8), :]
@@ -230,73 +259,68 @@
     total = lax.fori_loop(0, 16, squares, jnp.zeros((8, 128), jnp.float32))
     near[0] = jnp.sum(total, axis=0, keepdims=True)
 
-    def spread(buf, k, ids, send, recv):
+    def spread(buf, k, ids, n):
         return pltpu.make_async_remote_copy(
-            src_ref=buf.at[0], dst_ref=buf.at[k], send_sem=send.at[k], recv_sem=recv.at[k],
+            src_ref=buf.at[0], dst_ref=buf.at[k], send_sem=norm_send.at[n], recv_sem=norm_recv.at[n],
             device_id=ids[k], device_id_type=MESH,
         )
 
-    near_copies = [spread(near, k, near_ids, near_send, near_recv) for k in range(1, 16)]
-    far_copies = [spread(far, k, far_ids, far_send, far_recv) for k in range(1, 16)]
-    grads_1 = pair_copy(grads, cand_g.at[0], 3, "core")
-    grads_2 = pair_copy(grads, cand_g.at[1], 4, "zl")
-    grads_3 = pair_copy(cand_g.at[1], cand_g.at[2], 5, "core")
-    for c in near_copies:
-        c.start()
+    grads_1 = pair_copy(grads, cand_g.at[0], 2, "core")
+    grads_2 = pair_copy(grads, cand_g.at[2], 3, "zl")
+    grads_3 = pair_copy(cand_g.at[2], cand_g.at[1], 2, "core")
+    for k in range(1, 16):
+        spread(near, k, near_ids, 0).start()
     grads_1.start()
     grads_2.start()
-    for c in near_copies:
-        c.wait_recv()
+    wait_bytes(near.at[pl.ds(1, 15)], norm_recv.at[0])
     far[0] = functools.reduce(jnp.add, [near[k] for k in range(16)])
-    for c in far_copies:
-        c.start()
+    for k in range(1, 16):
+        spread(far, k, far_ids, 1).start()
     grads_2.wait_recv()
     grads_3.start()
-    for c in far_copies:
-        c.wait_recv()
-    norm2 = jnp.sum(functools.reduce(jnp.add, [far[k] for k in range(16)]), axis=1, keepdims=True)
+    wait_bytes(cand_g.at[pl.ds(0, 2)], pair_recv.at[2])
+    lax.fori_loop(0, 16, choose_grads, 0)
+
+    for part in range(3):
+        for phase in range(3):
+            sent = landing[part][phase] if phase < 2 else data[part][2].at[pl.ds(0, 3)]
+            wait_bytes(sent, ring_send.at[part * 3 + phase])
+    wait_bytes(cand, pair_send.at[0])
+    wait_bytes(cand_g, pair_send.at[1])
+    wait_bytes(near.at[pl.ds(1, 15)], norm_send.at[0])
+    wait_bytes(far.at[pl.ds(1, 15)], norm_send.at[1])
+    wait_bytes(far.at[pl.ds(1, 15)], norm_recv.at[1])
+    squares_sum[...] = functools.reduce(jnp.add, [far[k] for k in range(16)])
+
+
+def update_kernel(state, squares_sum, out_w, out_m, out_v, buf, sem):
+    norm2 = jnp.sum(squares_sum[...], axis=1, keepdims=True)
     scale = 1.0 / jnp.maximum(jnp.sqrt(norm2 / (4 * N_DP * SH)), 1.0)
-
-    shard_1.wait_recv()
-    shard_3.wait_recv()
-    grads_1.wait_recv()
-    grads_3.wait_recv()
-    mine = at["zl"] * 2 + at["core"]
-    mate = partner[0, mine]
-    apart = jnp.full((1, 1024), mine ^ mate, jnp.int32)
-    is_one, is_two = apart == 1, apart == 2
-    survive = jnp.full((1, 1024), mate - mine, jnp.int32) > 0
-
-    def update(i, carry):
-        cols = pl.ds(pl.multiple_of(i * 1024, 1024), 1024)
-        rows = pl.ds(pl.multiple_of(i * 8, 8), 8)
-
-        def chosen(one, two, three):
-            return jnp.where(is_one, one, jnp.where(is_two, two, three))
-
-        for slot in (0, 1):
-            if slot == 0:
-                weights, first, second = [own[a, :, cols] for a in range(3)]
-                total = grads[rows, :].reshape(1, 1024)
-            else:
-                weights, first, second = [chosen(*[cand[k, a, :, cols] for k in range(3)]) for a in range(3)]
-                total = chosen(*[cand_g[k, rows, :].reshape(1, 1024) for k in range(3)])
+    outs = (out_w, out_m, out_v)
+    n = SH // 4
+
+    def copies(q):
+        cols = pl.ds(pl.multiple_of(q * n, n), n)
+        return [pltpu.make_async_copy(buf.at[a, :, cols], outs[a].at[0, 0, :, cols], sem.at[a]) for a in range(3)]
+
+    def quarter(q, carry):
+        for i in range(n // 512):
+            cols = pl.ds(pl.multiple_of(q * n + i * 512, 512), 512)
+            weights, first, second, total = [state[a, :, cols] for a in range(4)]
             scaled = scale * total
             first_new = beta_one * first + (1.0 - beta_one) * scaled
             second_new = beta_two * second + (1.0 - beta_two) * scaled * scaled
             change = first_new / bias_one / (jnp.sqrt(second_new / bias_two) + eps_value) + decay * weights
-            for ref, value in ((out_w, weights - rate * change), (out_m, first_new), (out_v, second_new)):
-                ref[0, 0, slot : slot + 1, cols] = jnp.where(survive, value, 0.0)
+            buf[0, :, cols] = weights - rate * change
+            buf[1, :, cols] = first_new
+            buf[2, :, cols] = second_new
+        for c in copies(q):
+            c.start()
         return carry
 
-    lax.fori_loop(0, 16, update, 0)
-
-    for part in range(3):
-        for phase in range(3):
-            for kind in range(6):
-                ring(part, phase, kind).wait_send()
-    for c in [shard_1, shard_2, shard_3, grads_1, grads_2, grads_3] + near_copies + far_copies:
-        c.wait_send()
+    lax.fori_loop(0, 4, quarter, 0)
+    for a in range(3):
+        pltpu.make_async_copy(buf.at[a], outs[a].at[0, 0], sem.at[a]).wait()
 
 
 def on_device(master, moment1, moment2, local_grad, partner):
@@ -309,11 +333,11 @@
     vmem += [pltpu.VMEM((6, p[3], 128), f32) for p in PARTS]
     dma = pltpu.SemaphoreType.DMA
     out = jax.ShapeDtypeStruct((1, 1, 2, SH), f32)
-    return pl.pallas_call(
+    state, squares_sum = pl.pallas_call(
         kernel,
-        out_shape=(out, out, out),
+        out_shape=(pltpu.VMEM((4, 2, SH), f32), pltpu.VMEM((1, 128), f32)),
         in_specs=[pl.BlockSpec(memory_space=pltpu.SMEM)] + [pl.BlockSpec(memory_space=pltpu.HBM)] * 4,
-        out_specs=[pl.BlockSpec(memory_space=pltpu.VMEM)] * 3,
+        out_specs=[pl.BlockSpec(memory_space=pltpu.VMEM)] * 2,
         scratch_shapes=[
             pltpu.VMEM((1, N_DP * SH), jnp.bfloat16),
             pltpu.VMEM((3, 1, SH), f32),
@@ -324,11 +348,18 @@
             pltpu.VMEM((16, 1, 128), f32),
         ]
         + vmem
-        + [dma((4,)), dma((3,)), dma((54,)), dma((54,)), dma((6,)), dma((6,))]
-        + [dma((16,))] * 4,
+        + [dma((4,)), dma, dma((9,)), dma((27,)), dma((2,)), dma((4,)), dma((2,)), dma((2,))],
         compiler_params=pltpu.CompilerParams(collective_id=0, has_side_effects=True),
         name="step",
     )(partner, master, moment1, moment2, local_grad)
+    return pl.pallas_call(
+        update_kernel,
+        out_shape=(out, out, out),
+        in_specs=[pl.BlockSpec(memory_space=pltpu.VMEM)] * 2,
+        out_specs=[pl.BlockSpec(memory_space=pltpu.HBM)] * 3,
+        scratch_shapes=[pltpu.VMEM((3, 2, SH), f32), dma((3,))],
+        name="update",
+    )(*[pltpu.with_memory_space_constraint(v, pltpu.VMEM) for v in (state, squares_sum)])
 
 
 def solution(mesh):

time: 62.2 us -> 55.2 us (0.89)
  local copies, waits for them, and re-layouts: 4.7 us -> 0 us
  Pallas kernels: 56.7 us -> 54.5 us
    unnamed x3 -> x0, local copies, waits for them, and re-layouts: 4.7 us -> none
    pallas_call x1 -> x2, Pallas kernels: 56.7 us -> 54.5 us  [the longest x1 53.5 us: on_device(): pl.pallas_call(kernel, out_shape=(pltpu.VMEM((4, 2, SH), f32), pltpu.VMEM...]
where the time goes in v2:
time: 55.2 us; the launch traced here: 55.1 us
  Pallas kernels  54.5 us (99%)
  between operations  0.64 us (1%)
    pallas_call x1, Pallas kernels, on_device(): pl.pallas_call(kernel, out_shape=(pltpu.VMEM((4, 2, SH), f32), pltpu.VMEM...  53.5 us

profile of v2, /device:TPU:1, one launch (start us, length us, event | category | flops | bytes accessed | tf_op | source)
XLA Modules:
  0.0 55.1 jit_solution(6562533778947735367)
XLA Ops:
  0.6 53.5 %step.1 = (f32[4,2,16384]{2,1,0:T(2,128)S(1)}, f32[1,128]{1,0:T(1,128)S(1)}) custom-call(s32[1,4]{1,0:T(1,128)} %partner.1, f32[1,16384]{1,0:T(1,128)} %w_hbm.1, f32[1,16384]{1,0:T(1,128)} %m_hbm.1, f32[1,16384]{1,0:T(1,128)} %v_hbm.1, bf16[1,1,1048576]{2,1,0:T(2,128)(2,1)} %g_hbm.1), custom_call_target="tpu_custom_call" | custom-call | tf_op jit(solution)/shard_map/step/pallas_call | solution.py:336
  54.1 1.0 %update.1 = (f32[1,1,2,16384]{3,2,1,0:T(2,128)}, f32[1,1,2,16384]{3,2,1,0:T(2,128)}, f32[1,1,2,16384]{3,2,1,0:T(2,128)}) custom-call(f32[4,2,16384]{2,1,0:T(2,128)S(1)} %get-tuple-element.5.state, f32[1,128]{1,0:T(1,128)S(1)} %get-tuple-element.6.squares_sum), custom_call_target="tpu_custom_call" | custom-call | tf_op jit(solution)/shard_map/update/pallas_call | solution.py:355

commit v3 on v2

--- a/solution.py
+++ b/solution.py
@@ -63,9 +63,11 @@
         for k in range(16)
     ]
     far_ids = [{"x": beside("x", k // 4), "y": beside("y", k % 4)} for k in range(16)]
-    for k in range(1, 16):
-        pl.semaphore_signal(barrier, inc=1, device_id=near_ids[k], device_id_type=MESH)
-        pl.semaphore_signal(barrier, inc=1, device_id=far_ids[k], device_id_type=MESH)
+    for axis in DP:
+        for step in (1, -1):
+            pl.semaphore_signal(barrier, inc=1, device_id={axis: beside(axis, step)}, device_id_type=MESH)
+    for axis in PAIR:
+        pl.semaphore_signal(barrier, inc=1, device_id={axis: 1 - at[axis]}, device_id_type=MESH)
 
     def convert(part, c0, half):
         order, row, rows, _ = PARTS[part]
@@ -183,7 +185,7 @@
         convert(part, beside(axis, 2), 0)
         convert(part, beside(axis, 2), 1)
         if part == 0:
-            pl.semaphore_wait(barrier, 30)
+            pl.semaphore_wait(barrier, 8)
         ring(part, 0, AP).start()
         ring(part, 0, AM).start()
     for part in (0, 1, 2):
@@ -211,8 +213,6 @@
     shard_1 = pair_copy(own, cand.at[0], 0, "core")
     shard_2 = pair_copy(own, cand.at[2], 1, "zl")
     shard_3 = pair_copy(cand.at[2], cand.at[1], 0, "core")
-    shard_1.start()
-    shard_2.start()
 
     mine = at["zl"] * 2 + at["core"]
     mate = partner[0, mine]
@@ -242,6 +242,9 @@
             close_phase(part, phase)
             if phase < 2:
                 open_phase(part, phase + 1)
+            if phase == 0 and part == FIRST[0]:
+                shard_1.start()
+                shard_2.start()
         if phase < 2:
             for part in FIRST:
                 forward(part, phase + 1)

time: 55.2 us -> 54 us (0.978)
  Pallas kernels: 54.5 us -> 53.3 us
    pallas_call x1, Pallas kernels: 53.5 us -> 52.3 us  [on_device(): pl.pallas_call(kernel, out_shape=(pltpu.VMEM((4, 2, SH), f32), pltpu.VMEM...]
where the time goes in v3:
time: 54 us; the launch traced here: 53.9 us
  Pallas kernels  53.3 us (99%)
  between operations  0.64 us (1%)
    pallas_call x1, Pallas kernels, on_device(): pl.pallas_call(kernel, out_shape=(pltpu.VMEM((4, 2, SH), f32), pltpu.VMEM...  52.3 us

profile of v3, /device:TPU:1, one launch (start us, length us, event | category | flops | bytes accessed | tf_op | source)
XLA Modules:
  0.0 53.9 jit_solution(7909489316755211106)
XLA Ops:
  0.6 52.3 %step.1 = (f32[4,2,16384]{2,1,0:T(2,128)S(1)}, f32[1,128]{1,0:T(1,128)S(1)}) custom-call(s32[1,4]{1,0:T(1,128)} %partner.1, f32[1,16384]{1,0:T(1,128)} %w_hbm.1, f32[1,16384]{1,0:T(1,128)} %m_hbm.1, f32[1,16384]{1,0:T(1,128)} %v_hbm.1, bf16[1,1,1048576]{2,1,0:T(2,128)(2,1)} %g_hbm.1), custom_call_target="tpu_custom_call" | custom-call | tf_op jit(solution)/shard_map/step/pallas_call | solution.py:339
  52.9 1.0 %update.1 = (f32[1,1,2,16384]{3,2,1,0:T(2,128)}, f32[1,1,2,16384]{3,2,1,0:T(2,128)}, f32[1,1,2,16384]{3,2,1,0:T(2,128)}) custom-call(f32[4,2,16384]{2,1,0:T(2,128)S(1)} %get-tuple-element.5.state, f32[1,128]{1,0:T(1,128)S(1)} %get-tuple-element.6.squares_sum), custom_call_target="tpu_custom_call" | custom-call | tf_op jit(solution)/shard_map/update/pallas_call | solution.py:358

commit v4 on v3

--- a/solution.py
+++ b/solution.py
@@ -23,23 +23,31 @@
 STRIDE = {"zh": 16, "x": 4, "y": 1}
 MESH = pl.DeviceIdType.MESH
 
+XYZ, YXZ, ZXY, ZYX = ("x", "y", "zh"), ("y", "x", "zh"), ("zh", "x", "y"), ("zh", "y", "x")
 PARTS = (
-    (("x", "y", "zh"), 0, 56, 32),
-    (("y", "x", "zh"), 56, 56, 32),
-    (("zh", "x", "y"), 112, 16, 8),
+    (ZXY, 12, 8),
+    (ZYX, 12, 8),
+    (XYZ, 32, 16),
+    (YXZ, 32, 16),
+    (XYZ, 20, 12),
+    (YXZ, 20, 12),
 )
-FIRST = (2, 0, 1)
+START = tuple(sum(p[1] for p in PARTS[:i]) for i in range(len(PARTS)))
+EARLY = 4
+LOADING = (2, 3, 0, 1) + tuple(range(4, len(PARTS)))
+ORDER_A = (2,3,4,5,0,1)
+ORDER_SUM = (2,3,0,1,4,5)
+ORDER_LATER = (0,1,2,3,4,5)
 AP, AM, BP, BM, CP, CM = range(6)
 
 
 def kernel(
     partner, w_hbm, m_hbm, v_hbm, g_hbm, state, squares_sum,
     stage, own, cand, grads, cand_g, near, far,
-    f0, f1, f2, r0, r1, r2, s0, s1, s2, q0, q1, q2, t0, t1, t2, u0, u1, u2,
-    load_sem, own_sem, ring_send, ring_recv, pair_send, pair_recv, norm_send, norm_recv,
+    load_sem, own_sem, ring_send, ring_recv, pair_send, pair_recv, norm_send, norm_recv, *ring_bufs,
 ):
-    data = ((f0, s0, t0), (f1, s1, t1), (f2, s2, t2))
-    landing = ((r0, q0, u0), (r1, q1, u1), (r2, q2, u2))
+    data = [ring_bufs[6 * p : 6 * p + 3] for p in range(len(PARTS))]
+    landing = [ring_bufs[6 * p + 3 : 6 * p + 6] for p in range(len(PARTS))]
     at = {a: lax.axis_index(a) for a in PAIR + DP}
 
     def beside(axis, step):
@@ -69,34 +77,34 @@
     for axis in PAIR:
         pl.semaphore_signal(barrier, inc=1, device_id={axis: 1 - at[axis]}, device_id_type=MESH)
 
+    def pieces(width):
+        return [pl.ds(lo, min(1024, width - lo)) for lo in range(0, width, 1024)]
+
     def convert(part, c0, half):
-        order, row, rows, _ = PARTS[part]
+        order, rows, _ = PARTS[part]
         dst = data[part][0]
-
-        def body(i, carry):
-            c1 = half * 2 + i // 4
-            c2 = lax.rem(i, 4)
-            block = c0 * STRIDE[order[0]] + c1 * STRIDE[order[1]] + c2 * STRIDE[order[2]]
-            for j in range(rows // 8):
-                piece = stage[0:1, pl.ds(pl.multiple_of(block * SH + (row + 8 * j) * 128, 1024), 1024)]
-                dst[c0, c1, c2, pl.ds(8 * j, 8), :] = piece.astype(jnp.float32).reshape(8, 128)
-            return carry
-
-        lax.fori_loop(0, 8, body, 0)
+        for c1 in (2 * half, 2 * half + 1):
+
+            def body(c2, carry, c1=c1):
+                block = c0 * STRIDE[order[0]] + c1 * STRIDE[order[1]] + c2 * STRIDE[order[2]]
+                for p in pieces(rows * 128):
+                    cols = pl.ds(pl.multiple_of(block * SH + START[part] * 128 + p.start, 128), p.size)
+                    dst[c0, c1, c2, :, p] = stage[0:1, cols].astype(jnp.float32)
+                return carry
+
+            lax.fori_loop(0, 4, body, 0)
+
+    def halves(part):
+        rows, cut = PARTS[part][1:]
+        return pl.ds(0, cut * 128), pl.ds(cut * 128, (rows - cut) * 128)
 
     def view(part, phase, c, half):
         ref = data[part][phase]
-        if phase < 2:
-            return ref.at[c, pl.ds(2 * half, 2)]
-        cut, rows = PARTS[part][3], PARTS[part][2]
-        return ref.at[c, pl.ds(0, cut)] if half == 0 else ref.at[c, pl.ds(cut, rows - cut)]
+        return ref.at[c, pl.ds(2 * half, 2)] if phase < 2 else ref.at[c, :, halves(part)[half]]
 
     def landed(part, phase, kind, half):
         ref = landing[part][phase].at[kind]
-        if phase < 2:
-            return ref
-        cut, rows = PARTS[part][3], PARTS[part][2]
-        return ref.at[pl.ds(0, cut if half == 0 else rows - cut)]
+        return ref if phase < 2 else ref.at[:, pl.ds(0, halves(part)[half].size)]
 
     HALF = {AP: 0, AM: 1, BP: 1, BM: 0, CP: 0, CM: 1}
     CHUNK = {AP: 2, AM: -2, BP: 1, BM: -1, CP: 1, CM: -1}
@@ -116,38 +124,28 @@
     def wait_bytes(ref, sem):
         pltpu.make_async_copy(ref, ref, sem).wait()
 
-    def flat(ref):
-        shape = ref.shape
-        rows = shape[-2] // 8
-        lead = [()]
-        for n in shape[:-2]:
-            lead = [i + (j,) for i in lead for j in range(n)]
-        return lead, rows
-
     def add_up(dst, *srcs):
-        lead, rows = flat(dst)
-        if len(lead) > 2:
-            n1 = dst.shape[1]
+        lead, width = dst.shape[:-2], dst.shape[-1]
+
+        def one(idx):
+            for p in pieces(width):
+                at_p = idx + (slice(None), p)
+                total = srcs[0][at_p]
+                for s in srcs[1:]:
+                    total = total + s[at_p]
+                dst[at_p] = total
+
+        if len(lead) == 2:
 
             def body(i, carry):
-                idx = (i // n1, lax.rem(i, n1))
-                for j in range(rows):
-                    tile = idx + (pl.ds(8 * j, 8), slice(None))
-                    total = srcs[0][tile]
-                    for s in srcs[1:]:
-                        total = total + s[tile]
-                    dst[tile] = total
+                for j in range(lead[0]):
+                    one((j, i))
                 return carry
 
-            lax.fori_loop(0, len(lead), body, 0)
+            lax.fori_loop(0, lead[1], body, 0)
         else:
-            for idx in lead:
-                for j in range(rows):
-                    tile = idx + (pl.ds(8 * j, 8), slice(None))
-                    total = srcs[0][tile]
-                    for s in srcs[1:]:
-                        total = total + s[tile]
-                    dst[tile] = total
+            for j in range(lead[0] if lead else 1):
+                one((j,) if lead else ())
 
     def open_phase(part, phase):
         for kind in (AP, AM, BP, BM):
@@ -174,34 +172,35 @@
             if phase < 2:
                 add_up(data[part][phase + 1].at[pl.ds(2 * half, 2)], *srcs)
             else:
-                row, rows, cut = PARTS[part][1:]
-                lo, n = (0, cut) if half == 0 else (cut, rows - cut)
-                add_up(grads.at[pl.ds(row + lo, n)], *srcs)
-
-    for part in (0, 1, 2):
+                cols = halves(part)[half]
+                add_up(grads.at[:, pl.ds(START[part] * 128 + cols.start, cols.size)], *srcs)
+
+    for n, part in enumerate(LOADING):
         axis = PARTS[part][0][0]
-        for i in groups[:1] if part == 0 else groups[1:] if part == 1 else ():
+        for i in (groups[:1], groups[1:])[n] if n < 2 else ():
             loaded(i)
         convert(part, beside(axis, 2), 0)
         convert(part, beside(axis, 2), 1)
-        if part == 0:
+        if n == 0:
             pl.semaphore_wait(barrier, 8)
         ring(part, 0, AP).start()
         ring(part, 0, AM).start()
-    for part in (0, 1, 2):
+    for part in LOADING:
         axis = PARTS[part][0][0]
         convert(part, beside(axis, 1), 1)
         convert(part, beside(axis, -1), 0)
         ring(part, 0, BP).start()
         ring(part, 0, BM).start()
-    for part in FIRST:
+    for part in LOADING:
         axis = PARTS[part][0][0]
         convert(part, beside(axis, 1), 0)
         convert(part, beside(axis, -1), 1)
+    for part in ORDER_A:
+        forward(part, 0)
+    for part in LOADING:
+        axis = PARTS[part][0][0]
         convert(part, at[axis], 0)
         convert(part, at[axis], 1)
-    for part in FIRST:
-        forward(part, 0)
 
     def pair_copy(src, dst, n, axis):
         return pltpu.make_async_remote_copy(
@@ -233,20 +232,31 @@
 
     def choose_grads(i, carry):
         cols = pl.ds(pl.multiple_of(i * 1024, 1024), 1024)
-        rows = pl.ds(pl.multiple_of(i * 8, 8), 8)
-        keep(3, cols, grads[rows, :].reshape(1, 1024), [cand_g[k, rows, :].reshape(1, 1024) for k in (0, 2, 1)])
+        keep(3, cols, grads[:, cols], [cand_g[k, :, cols] for k in (0, 2, 1)])
         return carry
 
+    early = START[EARLY] * 128
+    shares = (pl.ds(0, early), pl.ds(early, SH - early))
+
+    def grads_copy(step, share):
+        src = cand_g.at[2] if step == 2 else grads
+        return pair_copy(
+            src.at[:, shares[share]], cand_g.at[(0, 2, 1)[step], :, shares[share]], 2 + 2 * share + step % 2, ("core", "zl", "core")[step]
+        )
+
     for phase in (0, 1, 2):
-        for part in FIRST:
+        for part in ORDER_LATER if phase else ORDER_SUM:
             close_phase(part, phase)
             if phase < 2:
                 open_phase(part, phase + 1)
-            if phase == 0 and part == FIRST[0]:
+            elif part == EARLY - 1:
+                grads_copy(0, 0).start()
+                grads_copy(1, 0).start()
+            if phase == 0 and part == 1:
                 shard_1.start()
                 shard_2.start()
         if phase < 2:
-            for part in FIRST:
+            for part in ORDER_LATER:
                 forward(part, phase + 1)
         if phase == 0:
             shard_2.wait_recv()
@@ -256,11 +266,11 @@
             lax.fori_loop(0, 16, choose, 0)
 
     def squares(i, total):
-        tile = grads[pl.ds(pl.multiple_of(i * 8, 8), 8), :]
+        tile = grads[:, pl.ds(pl.multiple_of(i * 1024, 1024), 1024)]
         return total + tile * tile
 
-    total = lax.fori_loop(0, 16, squares, jnp.zeros((8, 128), jnp.float32))
-    near[0] = jnp.sum(total, axis=0, keepdims=True)
+    total = lax.fori_loop(0, 16, squares, jnp.zeros((1, 1024), jnp.float32))
+    near[0] = jnp.sum(total.reshape(8, 128), axis=0, keepdims=True)
 
     def spread(buf, k, ids, n):
         return pltpu.make_async_remote_copy(
@@ -268,28 +278,29 @@
             device_id=ids[k], device_id_type=MESH,
         )
 
-    grads_1 = pair_copy(grads, cand_g.at[0], 2, "core")
-    grads_2 = pair_copy(grads, cand_g.at[2], 3, "zl")
-    grads_3 = pair_copy(cand_g.at[2], cand_g.at[1], 2, "core")
     for k in range(1, 16):
         spread(near, k, near_ids, 0).start()
-    grads_1.start()
-    grads_2.start()
+    grads_copy(0, 1).start()
+    grads_copy(1, 1).start()
+    grads_copy(1, 0).wait_recv()
+    grads_copy(2, 0).start()
     wait_bytes(near.at[pl.ds(1, 15)], norm_recv.at[0])
     far[0] = functools.reduce(jnp.add, [near[k] for k in range(16)])
     for k in range(1, 16):
         spread(far, k, far_ids, 1).start()
-    grads_2.wait_recv()
-    grads_3.start()
-    wait_bytes(cand_g.at[pl.ds(0, 2)], pair_recv.at[2])
+    grads_copy(1, 1).wait_recv()
+    grads_copy(2, 1).start()
+    for share in (0, 1):
+        wait_bytes(cand_g.at[pl.ds(0, 2), :, shares[share]], pair_recv.at[2 + 2 * share])
     lax.fori_loop(0, 16, choose_grads, 0)
 
-    for part in range(3):
+    for part in range(len(PARTS)):
         for phase in range(3):
             sent = landing[part][phase] if phase < 2 else data[part][2].at[pl.ds(0, 3)]
             wait_bytes(sent, ring_send.at[part * 3 + phase])
     wait_bytes(cand, pair_send.at[0])
-    wait_bytes(cand_g, pair_send.at[1])
+    for share in (0, 1):
+        wait_bytes(cand_g.at[:, :, shares[share]], pair_send.at[1 + share])
     wait_bytes(near.at[pl.ds(1, 15)], norm_send.at[0])
     wait_bytes(far.at[pl.ds(1, 15)], norm_send.at[1])
     wait_bytes(far.at[pl.ds(1, 15)], norm_recv.at[1])
@@ -328,12 +339,10 @@
 
 def on_device(master, moment1, moment2, local_grad, partner):
     f32 = jnp.float32
-    vmem = [pltpu.VMEM((4, 4, 4, p[2], 128), f32) for p in PARTS]
-    vmem += [pltpu.VMEM((6, 2, 4, p[2], 128), f32) for p in PARTS]
-    vmem += [pltpu.VMEM((4, 4, p[2], 128), f32) for p in PARTS]
-    vmem += [pltpu.VMEM((6, 2, p[2], 128), f32) for p in PARTS]
-    vmem += [pltpu.VMEM((4, p[2], 128), f32) for p in PARTS]
-    vmem += [pltpu.VMEM((6, p[3], 128), f32) for p in PARTS]
+    vmem = []
+    for _, rows, cut in PARTS:
+        vmem += [pltpu.VMEM(n + (1, rows * 128), f32) for n in ((4, 4, 4), (4, 4), (4,), (6, 2, 4), (6, 2))]
+        vmem.append(pltpu.VMEM((6, 1, max(cut, rows - cut) * 128), f32))
     dma = pltpu.SemaphoreType.DMA
     out = jax.ShapeDtypeStruct((1, 1, 2, SH), f32)
     state, squares_sum = pl.pallas_call(
@@ -345,13 +354,13 @@
             pltpu.VMEM((1, N_DP * SH), jnp.bfloat16),
             pltpu.VMEM((3, 1, SH), f32),
             pltpu.VMEM((3, 3, 1, SH), f32),
-            pltpu.VMEM((128, 128), f32),
-            pltpu.VMEM((3, 128, 128), f32),
+            pltpu.VMEM((1, SH), f32),
+            pltpu.VMEM((3, 1, SH), f32),
             pltpu.VMEM((16, 1, 128), f32),
             pltpu.VMEM((16, 1, 128), f32),
         ]
-        + vmem
-        + [dma((4,)), dma, dma((9,)), dma((27,)), dma((2,)), dma((4,)), dma((2,)), dma((2,))],
+        + [dma((4,)), dma, dma((3 * len(PARTS),)), dma((9 * len(PARTS),)), dma((3,)), dma((6,)), dma((2,)), dma((2,))]
+        + vmem,
         compiler_params=pltpu.CompilerParams(collective_id=0, has_side_effects=True),
         name="step",
     )(partner, master, moment1, moment2, local_grad)

time: 54 us -> 52.2 us (0.967)
  Pallas kernels: 53.3 us -> 51.4 us
    pallas_call x1, Pallas kernels: 52.3 us -> 50.5 us  [on_device(): pl.pallas_call(kernel, out_shape=(pltpu.VMEM((4, 2, SH), f32), pltpu.VMEM...]
where the time goes in v4:
time: 52.2 us; the launch traced here: 52.1 us
  Pallas kernels  51.4 us (98%)
  between operations  0.64 us (1%)
    pallas_call x1, Pallas kernels, on_device(): pl.pallas_call(kernel, out_shape=(pltpu.VMEM((4, 2, SH), f32), pltpu.VMEM...  50.5 us

profile of v4, /device:TPU:1, one launch (start us, length us, event | category | flops | bytes accessed | tf_op | source)
XLA Modules:
  0.0 52.1 jit_solution(16196528594131075025)
XLA Ops:
  0.6 50.5 %step.1 = (f32[4,2,16384]{2,1,0:T(2,128)S(1)}, f32[1,128]{1,0:T(1,128)S(1)}) custom-call(s32[1,4]{1,0:T(1,128)} %partner.1, f32[1,16384]{1,0:T(1,128)} %w_hbm.1, f32[1,16384]{1,0:T(1,128)} %m_hbm.1, f32[1,16384]{1,0:T(1,128)} %v_hbm.1, bf16[1,1,1048576]{2,1,0:T(2,128)(2,1)} %g_hbm.1), custom_call_target="tpu_custom_call" | custom-call | tf_op jit(solution)/shard_map/step/pallas_call | solution.py:348
  51.1 1.0 %update.1 = (f32[1,1,2,16384]{3,2,1,0:T(2,128)}, f32[1,1,2,16384]{3,2,1,0:T(2,128)}, f32[1,1,2,16384]{3,2,1,0:T(2,128)}) custom-call(f32[4,2,16384]{2,1,0:T(2,128)S(1)} %get-tuple-element.5.state, f32[1,128]{1,0:T(1,128)S(1)} %get-tuple-element.6.squares_sum), custom_call_target="tpu_custom_call" | custom-call | tf_op jit(solution)/shard_map/update/pallas_call | solution.py:367

commit v5 on v4

--- a/solution.py
+++ b/solution.py
@@ -25,26 +25,30 @@
 
 XYZ, YXZ, ZXY, ZYX = ("x", "y", "zh"), ("y", "x", "zh"), ("zh", "x", "y"), ("zh", "y", "x")
 PARTS = (
-    (ZXY, 12, 8),
-    (ZYX, 12, 8),
-    (XYZ, 32, 16),
-    (YXZ, 32, 16),
-    (XYZ, 20, 12),
-    (YXZ, 20, 12),
+    (ZXY, 12, 8, False),
+    (ZYX, 12, 8, False),
+    (XYZ, 24, 12, False),
+    (YXZ, 24, 12, False),
+    (XYZ, 16, 8, False),
+    (YXZ, 16, 8, False),
+    (XYZ, 12, 8, True),
+    (YXZ, 12, 8, True),
 )
 START = tuple(sum(p[1] for p in PARTS[:i]) for i in range(len(PARTS)))
-EARLY = 4
+EARLY = 6
 LOADING = (2, 3, 0, 1) + tuple(range(4, len(PARTS)))
-ORDER_A = (2,3,4,5,0,1)
-ORDER_SUM = (2,3,0,1,4,5)
-ORDER_LATER = (0,1,2,3,4,5)
+ORDER_A = (2,3,4,5,0,1,6,7)
+ORDER_SUM = (2,3,0,1,4,5,6,7)
+ORDER_LATER = (2,3,0,1,4,5,6,7)
 AP, AM, BP, BM, CP, CM = range(6)
+RECV = [(i, phase, a) for i, p in enumerate(PARTS) for phase in range(3) for a in (True, False) if not (a and p[3] and phase)]
+RECV = {key: n for n, key in enumerate(RECV)}
 
 
 def kernel(
-    partner, w_hbm, m_hbm, v_hbm, g_hbm, state, squares_sum,
+    partner_hbm, w_hbm, m_hbm, v_hbm, g_hbm, state, squares_sum,
     stage, own, cand, grads, cand_g, near, far,
-    load_sem, own_sem, ring_send, ring_recv, pair_send, pair_recv, norm_send, norm_recv, *ring_bufs,
+    gauge, partner, partner_sem, load_sem, own_sem, ring_send, ring_recv, rest_send, pair_recv, norm_recv, *ring_bufs,
 ):
     data = [ring_bufs[6 * p : 6 * p + 3] for p in range(len(PARTS))]
     landing = [ring_bufs[6 * p + 3 : 6 * p + 6] for p in range(len(PARTS))]
@@ -60,6 +64,9 @@
             pltpu.make_async_copy(g_hbm.at[0, :, cols], stage.at[:, cols], load_sem.at[i % 4]).start()
     for i, ref in enumerate((w_hbm, m_hbm, v_hbm)):
         pltpu.make_async_copy(ref, own.at[i], own_sem).start()
+
+    partner_copy = pltpu.make_async_copy(partner_hbm, partner, partner_sem)
+    partner_copy.start()
 
     def loaded(i):
         part_of = stage.at[:, pl.ds(0, 16 * SH)]
@@ -81,7 +88,7 @@
         return [pl.ds(lo, min(1024, width - lo)) for lo in range(0, width, 1024)]
 
     def convert(part, c0, half):
-        order, rows, _ = PARTS[part]
+        order, rows = PARTS[part][:2]
         dst = data[part][0]
         for c1 in (2 * half, 2 * half + 1):
 
@@ -95,7 +102,7 @@
             lax.fori_loop(0, 4, body, 0)
 
     def halves(part):
-        rows, cut = PARTS[part][1:]
+        rows, cut = PARTS[part][1:3]
         return pl.ds(0, cut * 128), pl.ds(cut * 128, (rows - cut) * 128)
 
     def view(part, phase, c, half):
@@ -111,12 +118,11 @@
 
     def ring(part, phase, kind):
         axis = PARTS[part][0][phase]
-        n = part * 3 + phase
         return pltpu.make_async_remote_copy(
             src_ref=view(part, phase, beside(axis, CHUNK[kind]), HALF[kind]),
             dst_ref=landed(part, phase, kind, HALF[kind]),
-            send_sem=ring_send.at[n],
-            recv_sem=ring_recv.at[n * 3 + min(kind, BP)],
+            send_sem=ring_send,
+            recv_sem=ring_recv.at[RECV[part, phase, kind < BP]],
             device_id={axis: beside(axis, 1 if kind in (AP, BP, CP) else -1)},
             device_id_type=MESH,
         )
@@ -147,22 +153,50 @@
             for j in range(lead[0] if lead else 1):
                 one((j,) if lead else ())
 
+    def straight(part, phase, step):
+        axis = PARTS[part][0][phase]
+        there = beside(axis, step)
+        return pltpu.make_async_remote_copy(
+            src_ref=data[part][phase].at[there],
+            dst_ref=landing[part][phase].at[step - 1],
+            send_sem=ring_send,
+            recv_sem=ring_recv.at[RECV[part, phase, False]],
+            device_id={axis: there},
+            device_id_type=MESH,
+        )
+
+    def is_straight(part, phase):
+        return PARTS[part][3] and phase > 0
+
     def open_phase(part, phase):
+        if is_straight(part, phase):
+            for step in (2, 1, 3):
+                straight(part, phase, step).start()
+            return
         for kind in (AP, AM, BP, BM):
             ring(part, phase, kind).start()
 
     def forward(part, phase):
+        if is_straight(part, phase):
+            return
         axis = PARTS[part][0][phase]
+        arrived = data[part][2].at[0] if phase == 2 else landing[part][phase].at[pl.ds(0, 2)]
+        wait_bytes(arrived, ring_recv.at[RECV[part, phase, True]])
         for a, c in ((AP, CP), (AM, CM)):
-            ring(part, phase, a).wait_recv()
             mine = view(part, phase, beside(axis, CHUNK[c]), HALF[c])
             add_up(mine, mine, landed(part, phase, a, HALF[a]))
             ring(part, phase, c).start()
 
     def close_phase(part, phase):
         axis = PARTS[part][0][phase]
+        if is_straight(part, phase):
+            arrived = landing[part][phase]
+            wait_bytes(arrived, ring_recv.at[RECV[part, phase, False]])
+            out = data[part][2] if phase == 1 else grads.at[:, pl.ds(START[part] * 128, PARTS[part][1] * 128)]
+            add_up(out, data[part][phase].at[at[axis]], *[arrived.at[i] for i in range(3)])
+            return
         last = data[part][2].at[pl.ds(0, 2)]
-        wait_bytes(last if phase == 2 else landing[part][phase].at[pl.ds(2, 4)], ring_recv.at[(part * 3 + phase) * 3 + BP])
+        wait_bytes(last if phase == 2 else landing[part][phase].at[pl.ds(2, 4)], ring_recv.at[RECV[part, phase, False]])
         for half, b, c in ((0, BM, CP), (1, BP, CM)):
             srcs = (
                 view(part, phase, at[axis], half),
@@ -189,6 +223,8 @@
         axis = PARTS[part][0][0]
         convert(part, beside(axis, 1), 1)
         convert(part, beside(axis, -1), 0)
+        if PARTS[part][3]:
+            continue
         ring(part, 0, BP).start()
         ring(part, 0, BM).start()
     for part in LOADING:
@@ -196,6 +232,9 @@
         convert(part, beside(axis, 1), 0)
         convert(part, beside(axis, -1), 1)
     for part in ORDER_A:
+        if PARTS[part][3]:
+            ring(part, 0, BP).start()
+            ring(part, 0, BM).start()
         forward(part, 0)
     for part in LOADING:
         axis = PARTS[part][0][0]
@@ -204,7 +243,7 @@
 
     def pair_copy(src, dst, n, axis):
         return pltpu.make_async_remote_copy(
-            src_ref=src, dst_ref=dst, send_sem=pair_send.at[n // 2], recv_sem=pair_recv.at[n],
+            src_ref=src, dst_ref=dst, send_sem=rest_send, recv_sem=pair_recv.at[n],
             device_id={axis: 1 - at[axis]}, device_id_type=MESH,
         )
 
@@ -214,6 +253,7 @@
     shard_3 = pair_copy(cand.at[2], cand.at[1], 0, "core")
 
     mine = at["zl"] * 2 + at["core"]
+    partner_copy.wait()
     mate = partner[0, mine]
     apart = jnp.full((1, 1024), mine ^ mate, jnp.int32)
     is_one, is_two = apart == 1, apart == 2
@@ -249,7 +289,7 @@
             close_phase(part, phase)
             if phase < 2:
                 open_phase(part, phase + 1)
-            elif part == EARLY - 1:
+            elif part == [p for p in ORDER_LATER if p < EARLY][-1]:
                 grads_copy(0, 0).start()
                 grads_copy(1, 0).start()
             if phase == 0 and part == 1:
@@ -274,11 +314,11 @@
 
     def spread(buf, k, ids, n):
         return pltpu.make_async_remote_copy(
-            src_ref=buf.at[0], dst_ref=buf.at[k], send_sem=norm_send.at[n], recv_sem=norm_recv.at[n],
+            src_ref=buf.at[0], dst_ref=buf.at[k], send_sem=rest_send, recv_sem=norm_recv.at[n],
             device_id=ids[k], device_id_type=MESH,
         )
 
-    for k in range(1, 16):
+    for k in sorted(range(1, 16), key=lambda k: -min(k // 4, 4 - k // 4)):
         spread(near, k, near_ids, 0).start()
     grads_copy(0, 1).start()
     grads_copy(1, 1).start()
@@ -286,7 +326,7 @@
     grads_copy(2, 0).start()
     wait_bytes(near.at[pl.ds(1, 15)], norm_recv.at[0])
     far[0] = functools.reduce(jnp.add, [near[k] for k in range(16)])
-    for k in range(1, 16):
+    for k in sorted(range(1, 16), key=lambda k: -(min(k // 4, 4 - k // 4) + min(k % 4, 4 - k % 4))):
         spread(far, k, far_ids, 1).start()
     grads_copy(1, 1).wait_recv()
     grads_copy(2, 1).start()
@@ -294,15 +334,8 @@
         wait_bytes(cand_g.at[pl.ds(0, 2), :, shares[share]], pair_recv.at[2 + 2 * share])
     lax.fori_loop(0, 16, choose_grads, 0)
 
-    for part in range(len(PARTS)):
-        for phase in range(3):
-            sent = landing[part][phase] if phase < 2 else data[part][2].at[pl.ds(0, 3)]
-            wait_bytes(sent, ring_send.at[part * 3 + phase])
-    wait_bytes(cand, pair_send.at[0])
-    for share in (0, 1):
-        wait_bytes(cand_g.at[:, :, shares[share]], pair_send.at[1 + share])
-    wait_bytes(near.at[pl.ds(1, 15)], norm_send.at[0])
-    wait_bytes(far.at[pl.ds(1, 15)], norm_send.at[1])
+    wait_bytes(gauge.at[:, pl.ds(0, 63 * SH)], ring_send)
+    wait_bytes(gauge.at[:, pl.ds(0, 12 * SH + 30 * 128)], rest_send)
     wait_bytes(far.at[pl.ds(1, 15)], norm_recv.at[1])
     squares_sum[...] = functools.reduce(jnp.add, [far[k] for k in range(16)])
 
@@ -340,15 +373,15 @@
 def on_device(master, moment1, moment2, local_grad, partner):
     f32 = jnp.float32
     vmem = []
-    for _, rows, cut in PARTS:
-        vmem += [pltpu.VMEM(n + (1, rows * 128), f32) for n in ((4, 4, 4), (4, 4), (4,), (6, 2, 4), (6, 2))]
-        vmem.append(pltpu.VMEM((6, 1, max(cut, rows - cut) * 128), f32))
+    for _, rows, cut, straight in PARTS:
+        vmem += [pltpu.VMEM(n + (1, rows * 128), f32) for n in ((4, 4, 4), (4, 4), (4,), (6, 2, 4), (3, 4) if straight else (6, 2))]
+        vmem.append(pltpu.VMEM((3, 1, rows * 128) if straight else (6, 1, max(cut, rows - cut) * 128), f32))
     dma = pltpu.SemaphoreType.DMA
     out = jax.ShapeDtypeStruct((1, 1, 2, SH), f32)
     state, squares_sum = pl.pallas_call(
         kernel,
         out_shape=(pltpu.VMEM((4, 2, SH), f32), pltpu.VMEM((1, 128), f32)),
-        in_specs=[pl.BlockSpec(memory_space=pltpu.SMEM)] + [pl.BlockSpec(memory_space=pltpu.HBM)] * 4,
+        in_specs=[pl.BlockSpec(memory_space=pltpu.HBM)] * 5,
         out_specs=[pl.BlockSpec(memory_space=pltpu.VMEM)] * 2,
         scratch_shapes=[
             pltpu.VMEM((1, N_DP * SH), jnp.bfloat16),
@@ -358,8 +391,10 @@
             pltpu.VMEM((3, 1, SH), f32),
             pltpu.VMEM((16, 1, 128), f32),
             pltpu.VMEM((16, 1, 128), f32),
+            pltpu.VMEM((1, 63 * SH), f32),
         ]
-        + [dma((4,)), dma, dma((3 * len(PARTS),)), dma((9 * len(PARTS),)), dma((3,)), dma((6,)), dma((2,)), dma((2,))]
+        + [pltpu.SMEM((1, 4), jnp.int32), dma]
+        + [dma((4,)), dma, dma, dma((len(RECV),)), dma, dma((6,)), dma((2,))]
         + vmem,
         compiler_params=pltpu.CompilerParams(collective_id=0, has_side_effects=True),
         name="step",

time: 52.2 us -> 50.7 us (0.971)
  Pallas kernels: 51.4 us -> 49.9 us
    pallas_call x1, Pallas kernels: 50.5 us -> 49 us  [on_device(): pl.pallas_call(kernel, out_shape=(pltpu.VMEM((4, 2, SH), f32), pltpu.VMEM...]
where the time goes in v5:
time: 50.7 us; the launch traced here: 50.6 us
  Pallas kernels  49.9 us (98%)
  between operations  0.64 us (1%)
    pallas_call x1, Pallas kernels, on_device(): pl.pallas_call(kernel, out_shape=(pltpu.VMEM((4, 2, SH), f32), pltpu.VMEM...  49 us

profile of v5, /device:TPU:1, one launch (start us, length us, event | category | flops | bytes accessed | tf_op | source)
XLA Modules:
  0.0 50.6 jit_solution(11047234301919183847)
XLA Ops:
  0.6 49.0 %step.1 = (f32[4,2,16384]{2,1,0:T(2,128)S(1)}, f32[1,128]{1,0:T(1,128)S(1)}) custom-call(s32[1,4]{1,0:T(1,128)} %partner_hbm.1, f32[1,16384]{1,0:T(1,128)} %w_hbm.1, f32[1,16384]{1,0:T(1,128)} %m_hbm.1, f32[1,16384]{1,0:T(1,128)} %v_hbm.1, bf16[1,1,1048576]{2,1,0:T(2,128)(2,1)} %g_hbm.1), custom_call_target="tpu_custom_call" | custom-call | tf_op jit(solution)/shard_map/step/pallas_call | solution.py:381
  49.6 1.0 %update.1 = (f32[1,1,2,16384]{3,2,1,0:T(2,128)}, f32[1,1,2,16384]{3,2,1,0:T(2,128)}, f32[1,1,2,16384]{3,2,1,0:T(2,128)}) custom-call(f32[4,2,16384]{2,1,0:T(2,128)S(1)} %get-tuple-element.5.state, f32[1,128]{1,0:T(1,128)S(1)} %get-tuple-element.6.squares_sum), custom_call_target="tpu_custom_call" | custom-call | tf_op jit(solution)/shard_map/update/pallas_call | solution.py:402

commit v6 on v5

--- a/solution.py
+++ b/solution.py
@@ -25,23 +25,24 @@
 
 XYZ, YXZ, ZXY, ZYX = ("x", "y", "zh"), ("y", "x", "zh"), ("zh", "x", "y"), ("zh", "y", "x")
 PARTS = (
-    (ZXY, 12, 8, False),
-    (ZYX, 12, 8, False),
-    (XYZ, 24, 12, False),
-    (YXZ, 24, 12, False),
-    (XYZ, 16, 8, False),
-    (YXZ, 16, 8, False),
-    (XYZ, 12, 8, True),
-    (YXZ, 12, 8, True),
+    (ZXY, 12, 8, (2,)),
+    (ZYX, 12, 8, (2,)),
+    (XYZ, 24, 12, (2,)),
+    (YXZ, 24, 12, (2,)),
+    (XYZ, 16, 8, (2,)),
+    (YXZ, 16, 8, (2,)),
+    (XYZ, 12, 8, (1, 2)),
+    (YXZ, 12, 8, (1, 2)),
 )
 START = tuple(sum(p[1] for p in PARTS[:i]) for i in range(len(PARTS)))
+LATE = (6, 7,)
 EARLY = 6
 LOADING = (2, 3, 0, 1) + tuple(range(4, len(PARTS)))
 ORDER_A = (2,3,4,5,0,1,6,7)
 ORDER_SUM = (2,3,0,1,4,5,6,7)
 ORDER_LATER = (2,3,0,1,4,5,6,7)
 AP, AM, BP, BM, CP, CM = range(6)
-RECV = [(i, phase, a) for i, p in enumerate(PARTS) for phase in range(3) for a in (True, False) if not (a and p[3] and phase)]
+RECV = [(i, phase, a) for i, p in enumerate(PARTS) for phase in range(3) for a in (True, False) if not (a and phase in p[3])]
 RECV = {key: n for n, key in enumerate(RECV)}
 
 
@@ -166,7 +167,7 @@
         )
 
     def is_straight(part, phase):
-        return PARTS[part][3] and phase > 0
+        return phase in PARTS[part][3]
 
     def open_phase(part, phase):
         if is_straight(part, phase):
@@ -223,7 +224,7 @@
         axis = PARTS[part][0][0]
         convert(part, beside(axis, 1), 1)
         convert(part, beside(axis, -1), 0)
-        if PARTS[part][3]:
+        if part in LATE:
             continue
         ring(part, 0, BP).start()
         ring(part, 0, BM).start()
@@ -232,7 +233,7 @@
         convert(part, beside(axis, 1), 0)
         convert(part, beside(axis, -1), 1)
     for part in ORDER_A:
-        if PARTS[part][3]:
+        if part in LATE:
             ring(part, 0, BP).start()
             ring(part, 0, BM).start()
         forward(part, 0)
@@ -357,7 +358,7 @@
             scaled = scale * total
             first_new = beta_one * first + (1.0 - beta_one) * scaled
             second_new = beta_two * second + (1.0 - beta_two) * scaled * scaled
-            change = first_new / bias_one / (jnp.sqrt(second_new / bias_two) + eps_value) + decay * weights
+            change = first_new * (1.0 / bias_one) / (jnp.sqrt(second_new * (1.0 / bias_two)) + eps_value) + decay * weights
             buf[0, :, cols] = weights - rate * change
             buf[1, :, cols] = first_new
             buf[2, :, cols] = second_new
@@ -374,8 +375,8 @@
     f32 = jnp.float32
     vmem = []
     for _, rows, cut, straight in PARTS:
-        vmem += [pltpu.VMEM(n + (1, rows * 128), f32) for n in ((4, 4, 4), (4, 4), (4,), (6, 2, 4), (3, 4) if straight else (6, 2))]
-        vmem.append(pltpu.VMEM((3, 1, rows * 128) if straight else (6, 1, max(cut, rows - cut) * 128), f32))
+        vmem += [pltpu.VMEM(n + (1, rows * 128), f32) for n in ((4, 4, 4), (4, 4), (4,), (6, 2, 4), (3, 4) if 1 in straight else (6, 2))]
+        vmem.append(pltpu.VMEM((3, 1, rows * 128) if 2 in straight else (6, 1, max(cut, rows - cut) * 128), f32))
     dma = pltpu.SemaphoreType.DMA
     out = jax.ShapeDtypeStruct((1, 1, 2, SH), f32)
     state, squares_sum = pl.pallas_call(

time: 50.7 us -> 48.9 us (0.964)
  Pallas kernels: 49.9 us -> 48.2 us
    pallas_call x1, Pallas kernels: 49 us -> 47.2 us  [on_device(): pl.pallas_call(kernel, out_shape=(pltpu.VMEM((4, 2, SH), f32), pltpu.VMEM...]
where the time goes in v6:
time: 48.9 us; the launch traced here: 48.8 us
  Pallas kernels  48.2 us (99%)
  between operations  0.64 us (1%)
    pallas_call x1, Pallas kernels, on_device(): pl.pallas_call(kernel, out_shape=(pltpu.VMEM((4, 2, SH), f32), pltpu.VMEM...  47.2 us

profile of v6, /device:TPU:1, one launch (start us, length us, event | category | flops | bytes accessed | tf_op | source)
XLA Modules:
  0.0 48.8 jit_solution(4756096393870051988)
XLA Ops:
  0.6 47.2 %step.1 = (f32[4,2,16384]{2,1,0:T(2,128)S(1)}, f32[1,128]{1,0:T(1,128)S(1)}) custom-call(s32[1,4]{1,0:T(1,128)} %partner_hbm.1, f32[1,16384]{1,0:T(1,128)} %w_hbm.1, f32[1,16384]{1,0:T(1,128)} %m_hbm.1, f32[1,16384]{1,0:T(1,128)} %v_hbm.1, bf16[1,1,1048576]{2,1,0:T(2,128)(2,1)} %g_hbm.1), custom_call_target="tpu_custom_call" | custom-call | tf_op jit(solution)/shard_map/step/pallas_call | solution.py:382
  47.9 1.0 %update.1 = (f32[1,1,2,16384]{3,2,1,0:T(2,128)}, f32[1,1,2,16384]{3,2,1,0:T(2,128)}, f32[1,1,2,16384]{3,2,1,0:T(2,128)}) custom-call(f32[4,2,16384]{2,1,0:T(2,128)S(1)} %get-tuple-element.5.state, f32[1,128]{1,0:T(1,128)S(1)} %get-tuple-element.6.squares_sum), custom_call_target="tpu_custom_call" | custom-call | tf_op jit(solution)/shard_map/update/pallas_call | solution.py:403

commit v7 on v6

--- a/solution.py
+++ b/solution.py
@@ -27,10 +27,10 @@
 PARTS = (
     (ZXY, 12, 8, (2,)),
     (ZYX, 12, 8, (2,)),
-    (XYZ, 24, 12, (2,)),
-    (YXZ, 24, 12, (2,)),
-    (XYZ, 16, 8, (2,)),
-    (YXZ, 16, 8, (2,)),
+    (XYZ, 28, 16, (2,)),
+    (YXZ, 28, 16, (2,)),
+    (XYZ, 12, 8, (1, 2)),
+    (YXZ, 12, 8, (1, 2)),
     (XYZ, 12, 8, (1, 2)),
     (YXZ, 12, 8, (1, 2)),
 )

time: 48.9 us -> 48.6 us (level)
  no operation moved by 1% of the time
where the time goes in v7:
time: 48.6 us; the launch traced here: 48.5 us
  Pallas kernels  47.9 us (99%)
  between operations  0.64 us (1%)
    pallas_call x1, Pallas kernels, on_device(): pl.pallas_call(kernel, out_shape=(pltpu.VMEM((4, 2, SH), f32), pltpu.VMEM...  46.9 us

profile of v7, /device:TPU:1, one launch (start us, length us, event | category | flops | bytes accessed | tf_op | source)
XLA Modules:
  0.0 48.5 jit_solution(15154413089206367487)
XLA Ops:
  0.6 46.9 %step.1 = (f32[4,2,16384]{2,1,0:T(2,128)S(1)}, f32[1,128]{1,0:T(1,128)S(1)}) custom-call(s32[1,4]{1,0:T(1,128)} %partner_hbm.1, f32[1,16384]{1,0:T(1,128)} %w_hbm.1, f32[1,16384]{1,0:T(1,128)} %m_hbm.1, f32[1,16384]{1,0:T(1,128)} %v_hbm.1, bf16[1,1,1048576]{2,1,0:T(2,128)(2,1)} %g_hbm.1), custom_call_target="tpu_custom_call" | custom-call | tf_op jit(solution)/shard_map/step/pallas_call | solution.py:382
  47.5 1.0 %update.1 = (f32[1,1,2,16384]{3,2,1,0:T(2,128)}, f32[1,1,2,16384]{3,2,1,0:T(2,128)}, f32[1,1,2,16384]{3,2,1,0:T(2,128)}) custom-call(f32[4,2,16384]{2,1,0:T(2,128)S(1)} %get-tuple-element.5.state, f32[1,128]{1,0:T(1,128)S(1)} %get-tuple-element.6.squares_sum), custom_call_target="tpu_custom_call" | custom-call | tf_op jit(solution)/shard_map/update/pallas_call | solution.py:403

commit v8 on v7

--- a/solution.py
+++ b/solution.py
@@ -307,10 +307,10 @@
             lax.fori_loop(0, 16, choose, 0)
 
     def squares(i, total):
-        tile = grads[:, pl.ds(pl.multiple_of(i * 1024, 1024), 1024)]
+        tile = grads[:, pl.ds(i * 1024, 1024)]
         return total + tile * tile
 
-    total = lax.fori_loop(0, 16, squares, jnp.zeros((1, 1024), jnp.float32))
+    total = functools.reduce(lambda t, i: squares(i, t), range(16), jnp.zeros((1, 1024), jnp.float32))
     near[0] = jnp.sum(total.reshape(8, 128), axis=0, keepdims=True)
 
     def spread(buf, k, ids, n):

time: 48.6 us -> 48.5 us (level)
  no operation moved by 1% of the time
where the time goes in v8:
time: 48.5 us; the launch traced here: 48.4 us
  Pallas kernels  47.8 us (99%)
  between operations  0.64 us (1%)
    pallas_call x1, Pallas kernels, on_device(): pl.pallas_call(kernel, out_shape=(pltpu.VMEM((4, 2, SH), f32), pltpu.VMEM...  46.8 us

profile of v8, /device:TPU:1, one launch (start us, length us, event | category | flops | bytes accessed | tf_op | source)
XLA Modules:
  0.0 48.4 jit_solution(10269328866119407657)
XLA Ops:
  0.6 46.8 %step.1 = (f32[4,2,16384]{2,1,0:T(2,128)S(1)}, f32[1,128]{1,0:T(1,128)S(1)}) custom-call(s32[1,4]{1,0:T(1,128)} %partner_hbm.1, f32[1,16384]{1,0:T(1,128)} %w_hbm.1, f32[1,16384]{1,0:T(1,128)} %m_hbm.1, f32[1,16384]{1,0:T(1,128)} %v_hbm.1, bf16[1,1,1048576]{2,1,0:T(2,128)(2,1)} %g_hbm.1), custom_call_target="tpu_custom_call" | custom-call | tf_op jit(solution)/shard_map/step/pallas_call | solution.py:382
  47.5 1.0 %update.1 = (f32[1,1,2,16384]{3,2,1,0:T(2,128)}, f32[1,1,2,16384]{3,2,1,0:T(2,128)}, f32[1,1,2,16384]{3,2,1,0:T(2,128)}) custom-call(f32[4,2,16384]{2,1,0:T(2,128)S(1)} %get-tuple-element.5.state, f32[1,128]{1,0:T(1,128)S(1)} %get-tuple-element.6.squares_sum), custom_call_target="tpu_custom_call" | custom-call | tf_op jit(solution)/shard_map/update/pallas_call | solution.py:403

commit v9 on v8

--- a/solution.py
+++ b/solution.py
@@ -36,7 +36,7 @@
 )
 START = tuple(sum(p[1] for p in PARTS[:i]) for i in range(len(PARTS)))
 LATE = (6, 7,)
-EARLY = 6
+EARLY = 4
 LOADING = (2, 3, 0, 1) + tuple(range(4, len(PARTS)))
 ORDER_A = (2,3,4,5,0,1,6,7)
 ORDER_SUM = (2,3,0,1,4,5,6,7)

time: 48.5 us -> 48.6 us (level)
  no operation moved by 1% of the time
where the time goes in v9:
time: 48.6 us; the launch traced here: 48.5 us
  Pallas kernels  47.9 us (99%)
  between operations  0.64 us (1%)
    pallas_call x1, Pallas kernels, on_device(): pl.pallas_call(kernel, out_shape=(pltpu.VMEM((4, 2, SH), f32), pltpu.VMEM...  46.9 us

profile of v9, /device:TPU:1, one launch (start us, length us, event | category | flops | bytes accessed | tf_op | source)
XLA Modules:
  0.0 48.5 jit_solution(12450604822538438947)
XLA Ops:
  0.6 46.9 %step.1 = (f32[4,2,16384]{2,1,0:T(2,128)S(1)}, f32[1,128]{1,0:T(1,128)S(1)}) custom-call(s32[1,4]{1,0:T(1,128)} %partner_hbm.1, f32[1,16384]{1,0:T(1,128)} %w_hbm.1, f32[1,16384]{1,0:T(1,128)} %m_hbm.1, f32[1,16384]{1,0:T(1,128)} %v_hbm.1, bf16[1,1,1048576]{2,1,0:T(2,128)(2,1)} %g_hbm.1), custom_call_target="tpu_custom_call" | custom-call | tf_op jit(solution)/shard_map/step/pallas_call | solution.py:382
  47.5 1.0 %update.1 = (f32[1,1,2,16384]{3,2,1,0:T(2,128)}, f32[1,1,2,16384]{3,2,1,0:T(2,128)}, f32[1,1,2,16384]{3,2,1,0:T(2,128)}) custom-call(f32[4,2,16384]{2,1,0:T(2,128)S(1)} %get-tuple-element.5.state, f32[1,128]{1,0:T(1,128)S(1)} %get-tuple-element.6.squares_sum), custom_call_target="tpu_custom_call" | custom-call | tf_op jit(solution)/shard_map/update/pallas_call | solution.py:403
